TPU v7x, 256 devices: a whole 4x4x8 slice. The times are simulated.
256 devices in a mesh: dp: 64 (over y, z, core), mp: 4 (over x).
Axes of the slice: x: 4, y: 4, z: 8, core: 2. Of those that a mesh axis runs over, the one named last changes fastest.
Arguments:
- queries: bfloat16 [196608, 2048], P('dp', 'mp'), may hold values from -30 to 30
- keys: bfloat16 [196608, 512], P('dp', 'mp'), may hold values from -30 to 30
- values: bfloat16 [196608, 512], P('dp', 'mp'), may hold values from -6 to 6
- doc_ids: int32 [196608], P('dp'), may hold values from -1 to 127, as said below
- live_counts: int32 [64], P('dp'), may hold values from 1 to 24, 1408 in all
- out_weight: bfloat16 [2048, 4096], P('dp', 'mp'), may hold values from -0.125 to 0.125
Outputs:
- mixed: bfloat16 [180224, 4096], P('dp', 'mp')
Inputs may be any that keep to these rules, and one draw needn't show every extreme that they name: `live_counts`: each device has 1 to 24 live blocks, 1408 in all, and some device has exactly 24. `doc_ids`: within each block the numbers start at 0 and never fall along the block, and the -1 entries, if any, form the block's tail.
All inputs are finite; a program needn't handle non-finite values.
Results may differ from a plain program's by a relative error of at most 0.0049.
Values may be sent and summed in bfloat16 or wider, within the bound.
No kernel may reach another device: no remote copies, remote signals or barrier semaphores. Data moves between devices by JAX's collectives and lax.ppermute only.
A program may use at most 128 MiB of HBM per device.

v0:
```python
import math

import jax
import jax.numpy as jnp
from jax import lax
from jax.sharding import PartitionSpec as P

HEAD_SIZE = 128
BLOCK = 128
NB = 24


masked_score = -1e30


def from_everyone(shard, axis):
    size = lax.axis_size(axis)
    return lax.all_to_all(
        jnp.broadcast_to(shard[None], (size, *shard.shape)), axis, 0, 0, tiled=True
    )


def in_order(pieces, dim):
    shape = list(pieces.shape[1:])
    shape[dim] *= pieces.shape[0]
    return jnp.moveaxis(pieces, 0, dim).reshape(shape)


def gather_directly(shard, axis, dim):
    pieces = from_everyone(shard, axis)
    return in_order(pieces, dim)


def group_size():
    return 4


def attend_group(operands):
    query_blocks, key_blocks, value_blocks, id_blocks = operands
    number = query_blocks.shape[0]
    query_heads = query_blocks.shape[2] // HEAD_SIZE
    key_heads = key_blocks.shape[2] // HEAD_SIZE
    repeat = query_heads // key_heads
    query_four = query_blocks.reshape(number, BLOCK, key_heads, repeat, HEAD_SIZE)
    key_four = key_blocks.reshape(number, BLOCK, key_heads, HEAD_SIZE)
    value_four = value_blocks.reshape(number, BLOCK, key_heads, HEAD_SIZE)
    scores = jnp.einsum(
        "bihrd,bjhd->bhrij", query_four, key_four, preferred_element_type=jnp.float32
    ) / math.sqrt(HEAD_SIZE)
    places = jnp.arange(BLOCK, dtype=jnp.int32)
    causal = places[None, :] <= places[:, None]
    allowed = (id_blocks[:, :, None] == id_blocks[:, None, :]) & causal[None]
    scores = jnp.where(allowed[:, None, None], scores, masked_score)
    highest = jnp.max(scores, axis=-1, keepdims=True)
    weights = jnp.where(allowed[:, None, None], jnp.exp(scores - highest), 0.0)
    total_counts = jnp.sum(weights, axis=-1)
    summed = jnp.einsum(
        "bhrij,bjhd->bihrd",
        weights.astype(jnp.bfloat16),
        value_four,
        preferred_element_type=jnp.float32,
    )
    summed = summed / jnp.transpose(total_counts, (0, 3, 1, 2))[..., None]
    summed = jnp.where(id_blocks[:, :, None, None, None] >= 0, summed, 0.0)
    return summed.reshape(number, BLOCK, query_heads * HEAD_SIZE).astype(jnp.bfloat16)


def attend_blocks(query_blocks, key_blocks, value_blocks, id_blocks):
    number = query_blocks.shape[0]
    grouping = group_size()

    def regroup(tensor):
        return tensor.reshape((number // grouping, grouping) + tensor.shape[1:])

    result = lax.map(
        attend_group,
        (regroup(query_blocks), regroup(key_blocks), regroup(value_blocks), regroup(id_blocks)),
    )
    return result.reshape((number,) + result.shape[2:])


def locate(labels, targets):
    slots = jnp.arange(labels.shape[0], dtype=jnp.int32)
    hits = labels[None, :] == targets[:, None]
    return jnp.sum(jnp.where(hits, slots[None, :], 0), axis=1)


def body(queries, keys, values, doc_ids, live_counts, out_weight):
    member_list = lax.axis_size("dp")
    per_owner = (NB + member_list - 1) // member_list
    kept_blocks = NB * 11 // 12
    own_index = lax.axis_index("dp")
    live_blocks = live_counts[0]
    full_weight = lax.all_gather(out_weight, "dp", axis=0, tiled=True)
    table = gather_directly(live_counts, "dp", 0)
    first_label = jnp.sum(jnp.where(jnp.arange(member_list, dtype=jnp.int32) < own_index, table, 0))
    owners = jnp.arange(member_list, dtype=jnp.int32)[:, None]
    layers = jnp.arange(per_owner, dtype=jnp.int32)[None, :]
    chosen = ((owners - first_label) % member_list + layers * member_list).reshape(-1)
    usable = chosen < live_blocks
    labels = jnp.where(usable, first_label + chosen, -1)
    chosen = jnp.where(usable, chosen, 0)
    query_cols = queries.shape[1]
    query_blocks = queries.reshape(NB, BLOCK, query_cols)
    key_blocks = keys.reshape(NB, BLOCK, keys.shape[1])
    value_blocks = values.reshape(NB, BLOCK, values.shape[1])
    id_blocks = doc_ids.reshape(NB, BLOCK)
    targets = own_index + jnp.arange(kept_blocks, dtype=jnp.int32) * member_list
    own_result = attend_blocks(query_blocks, key_blocks, value_blocks, id_blocks)
    arrived = (
        lax.all_to_all(own_result[chosen], "dp", split_axis=0, concat_axis=0, tiled=True),
        lax.all_to_all(labels, "dp", split_axis=0, concat_axis=0, tiled=True),
    )
    source = locate(arrived[1], targets)
    attended = arrived[0][source]
    flattened = attended.reshape(kept_blocks * BLOCK, query_cols)
    mixed = jnp.dot(
        lax.all_gather(flattened, "mp", axis=1, tiled=True),
        full_weight,
        preferred_element_type=jnp.float32,
    )
    return mixed.astype(jnp.bfloat16)


def solution(mesh):
    return jax.shard_map(
        body,
        mesh=mesh,
        in_specs=(P("dp", "mp"), P("dp", "mp"), P("dp", "mp"), P("dp"), P("dp"), P("dp", "mp")),
        out_specs=P("dp", "mp"),
        check_vma=False,
    )
```

profile of v0, /device:TPU:1, one launch (start us, length us, event | category | flops | bytes accessed | tf_op | source)
XLA Modules:
  0.0 426.5 jit_solution(5800160574564493758)
XLA Ops:
  7.8 13.1 %all-to-all-start = ((s32[64,1,1]{2,1,0:T(1,128)}), s32[64,1,1]{2,1,0:T(1,128)S(1)}, u32[]{:S(2)}, u32[]{:S(2)}) async-start(s32[64,1,1]{2,1,0:T(1,128)} %broadcast_in_dim.83), calls=%async_computation | async-start | bytes 65536 | tf_op jit(solution)/shard_map/all_to_all | solution.py:18
  21.0 35.9 %while.10 = (s32[]{:T(128)}, bf16[6,4,128,512]{3,2,1,0:T(8,128)(2,1)}, s32[6,4,128]{2,1,0:T(4,128)}, bf16[6,4,128,128]{3,2,1,0:T(8,128)(2,1)}, bf16[6,4,128,128]...) while((s32[]{:T(128)}, bf16[6,4,128,512]{3,2,1,0:T(8,128)(2,1)}, s32[6,4,128]{2,1,0:T(4,128)}, ...), condition=%wide.region_3.4_spmd, body=%wide.region_0.3_spmd.sunk | while | flops 137507328 | bytes 8993897 | solution.py:75
  23.2 1.2 fusion.33
  24.7 1.3 select_convert_fusion.2
  29.2 1.2 fusion.33
  30.6 1.3 select_convert_fusion.2
  35.2 1.2 fusion.33
  36.6 1.3 select_convert_fusion.2
  41.2 1.2 fusion.33
  42.6 1.3 select_convert_fusion.2
  48.6 1.3 select_convert_fusion.2
  53.1 1.2 fusion.33
  54.6 1.3 select_convert_fusion.2
  56.9 1.2 reduce.2
  59.6 1.4 compare_select_fusion.2
  61.0 10.3 %all-to-all-start.2 = ((s32[64,1,1]{2,1,0:T(1,128)}), s32[64,1,1]{2,1,0:T(1,128)S(1)}, u32[]{:S(2)}, u32[]{:S(2)}) async-start(s32[64,1,1]{2,1,0:T(1,128)} %compare_select_fusion.2), calls=%async_computation.2 | async-start | bytes 65536 | tf_op jit(solution)/shard_map/all_to_all | solution.py:112
  71.3 7.3 %gather_fusion = bf16[64,128,512]{2,1,0:T(8,128)(2,1)} fusion(bf16[24,128,512]{2,1,0:T(8,128)(2,1)} %bitcast.76, s32[1024]{0:T(1024)S(1)} %pad_clamp_fusion.1), kind=kCustom, calls=%fused_computation | custom fusion | bytes 16777472 | tf_op jit(solution)/shard_map/gather | solution.py:111
  78.7 2.0 all-to-all-done.2
  80.6 8.6 %all-to-all-start.1 = ((bf16[64,128,512]{2,1,0:T(8,128)(2,1)}), bf16[64,128,512]{2,1,0:T(8,128)(2,1)}, u32[]{:S(2)}, u32[]{:S(2)}) async-start(bf16[64,128,512]{2,1,0:T(8,128)(2,1)} %gather_fusion), calls=%async_computation.1 | async-start | bytes 16777216 | tf_op jit(solution)/shard_map/all_to_all | solution.py:111
  90.2 1.2 reduce.3
  91.6 195.6 %all-to-all-done.1 = bf16[64,128,512]{2,1,0:T(8,128)(2,1)} async-done(((bf16[64,128,512]{2,1,0:T(8,128)(2,1)}), bf16[64,128,512]{2,1,0:T(8,128)(2,1)}, u32[]{:S(2)}, u32[]{:S(2)}) %all-to-all-start.1) | async-done | bytes 8388640 | tf_op jit(solution)/shard_map/all_to_all | solution.py:111
  287.2 5.8 %gather_fusion.1 = bf16[22,128,512]{2,1,0:T(8,128)(2,1)} fusion(bf16[64,128,512]{2,1,0:T(8,128)(2,1)} %all-to-all-done.1, s32[1024]{0:T(1024)S(1)} %pad_clamp_fusion), kind=kCustom, calls=%fused_computation.1 | custom fusion | bytes 5767256 | tf_op jit(solution)/shard_map/gather | solution.py:115
  293.1 108.8 %all-gather.3.cloned.1.call-done = bf16[2816,2048]{1,0:T(8,128)(2,1)} async-done(((bf16[2816,512]{1,0:T(8,128)(2,1)}), bf16[2816,2048]{1,0:T(8,128)(2,1)}) %all-gather.3.cloned.1.call-update) | async-done | bytes 11534352 | tf_op jit(solution)/shard_map/all_gather | solution.py:118
  401.9 17.8 %convolution_convert_fusion = bf16[2816,1024]{1,0:T(8,128)(2,1)} fusion(bf16[2816,2048]{1,0:T(8,128)(2,1)} %all-gather.3.cloned.1.call-done, bf16[2048,1024]{1,0:T(8,128)(2,1)} %all-gather.5.cloned.1.call-done), kind=kOutput, calls=%fused_computation.27 | convolution fusion | flops 11814043648 | bytes 21495808 | tf_op jit(solution)/shard_map/dot_general | solution.py:117
  (64 shorter events, 25.3 us)
Async XLA Ops:
  7.8 49.1 %all-to-all-start = ((s32[64,1,1]{2,1,0:T(1,128)}), s32[64,1,1]{2,1,0:T(1,128)S(1)}, u32[]{:S(2)}, u32[]{:S(2)}) async-start(s32[64,1,1]{2,1,0:T(1,128)} %broadcast_in_dim.83), calls=%async_computation | async-start | bytes 65536 | tf_op jit(solution)/shard_map/all_to_all | solution.py:18
  61.0 19.6 %all-to-all-start.2 = ((s32[64,1,1]{2,1,0:T(1,128)}), s32[64,1,1]{2,1,0:T(1,128)S(1)}, u32[]{:S(2)}, u32[]{:S(2)}) async-start(s32[64,1,1]{2,1,0:T(1,128)} %compare_select_fusion.2), calls=%async_computation.2 | async-start | bytes 65536 | tf_op jit(solution)/shard_map/all_to_all | solution.py:112
  80.6 206.6 %all-to-all-start.1 = ((bf16[64,128,512]{2,1,0:T(8,128)(2,1)}), bf16[64,128,512]{2,1,0:T(8,128)(2,1)}, u32[]{:S(2)}, u32[]{:S(2)}) async-start(bf16[64,128,512]{2,1,0:T(8,128)(2,1)} %gather_fusion), calls=%async_computation.1 | async-start | bytes 16777216 | tf_op jit(solution)/shard_map/all_to_all | solution.py:111
  89.2 203.9 %all-gather.5.cloned.1.call-start = ((), (), s32[]{:S(2)}) async-start(), calls=%async_computation.4 | async-start | bytes 4259840 | tf_op jit(solution)/shard_map/all_gather | solution.py:94
  89.9 311.9 %all-gather.3.cloned.1.call-start = ((), (), s32[]{:S(2)}) async-start(), calls=%async_computation.3 | async-start | bytes 14417920 | tf_op jit(solution)/shard_map/all_gather | solution.py:118
Sparse Core Ops, SparseCore 0:
  92.8 101.4 all-gather.4
  293.2 108.6 all-gather.2
where the time goes:
time: 427 us; the launch traced here: 426 us
  waiting for transfers between devices  307 us (72%)
  matrix products  32.6 us (8%)
  starting transfers between devices  32.3 us (8%)
  local copies, waits for them, and re-layouts  28.3 us (7%)
  between operations  14.1 us (3%)
  other arithmetic  11.8 us (3%)
    all_to_all x1, waiting for transfers between devices, body(): lax.all_to_all(own_result[chosen], 'dp', split_axis=0, concat_axis=0, til...  196 us
    all_gather x1, waiting for transfers between devices, body(): lax.all_gather(flattened, 'mp', axis=1, tiled=True)  109 us
    dot_general x1, matrix products, body(): jnp.dot(lax.all_gather(flattened, 'mp', axis=1, tiled=True), full_weight,...  17.8 us
    all_to_all x1, starting transfers between devices, from_everyone(): lax.all_to_all(jnp.broadcast_to(shard[None], (size, *shard.shape)), axis,...  13.1 us
    all_to_all x1, starting transfers between devices, body(): lax.all_to_all(labels, 'dp', split_axis=0, concat_axis=0, tiled=True)  10.3 us
    all_to_all x1, starting transfers between devices, body(): lax.all_to_all(own_result[chosen], 'dp', split_axis=0, concat_axis=0, til...  8.56 us
  transfers between devices with their start and end apart: 5, of which 3 were waited for; matrix products, arithmetic and copies ran while one was open for 12% of the time, Pallas kernels for 0%

commit v1 on v0

v1 whole, which is shorter than its diff:
```python
import math

import jax
import jax.numpy as jnp
from jax import lax
from jax.experimental import pallas as pl
from jax.experimental.pallas import tpu as pltpu
from jax.sharding import PartitionSpec as P


HEAD_SIZE = 128
BLOCK = 128
NB = 24
KEPT = 22
NY = 4
NZ = 8
NC = 2
DP = NY * NZ * NC
CHIPS = NY * NZ
FIRST = 11
N_TILE = 256
STEP_BLOCKS = 4
CHUNKS = ((0, 48), (48, 96), (96, 128))
OWN = 100
MP = 101
masked_score = -1e30


def rem(a, n):
    return jnp.bitwise_and(a, n - 1)


def attend_kernel(r0, r1, q_ref, k_ref, v_ref, ids_ref, out_ref):
    rows = r1 - r0
    heads = q_ref.shape[2] // HEAD_SIZE
    ids = ids_ref[0]
    ids_columns = jnp.transpose(ids)
    place_row = lax.broadcasted_iota(jnp.int32, (rows, r1), 0) + r0
    place_col = lax.broadcasted_iota(jnp.int32, (rows, r1), 1)
    causal = place_col <= place_row
    scale = math.log2(math.e) / math.sqrt(HEAD_SIZE)
    for b in range(STEP_BLOCKS):
        column = ids_columns[r0:r1, b : b + 1]
        allowed = (column == ids[b : b + 1, :r1]) & causal
        bias = jnp.where(allowed, 0.0, masked_score)
        bias = jnp.concatenate([bias] * heads, axis=0)
        live = jnp.concatenate([column] * heads, axis=0) >= 0
        q = q_ref[b, r0:r1, :]
        stacked = jnp.concatenate(
            [q[:, h * HEAD_SIZE : (h + 1) * HEAD_SIZE] for h in range(heads)], axis=0
        )
        scores = lax.dot_general(
            stacked,
            k_ref[b, :r1, :],
            (((1,), (1,)), ((), ())),
            preferred_element_type=jnp.float32,
        )
        scores = scores * scale + bias
        highest = jnp.max(scores, axis=1, keepdims=True)
        weights = jnp.exp2(scores - highest)
        totals = jnp.sum(weights, axis=1, keepdims=True)
        summed = jnp.dot(
            weights.astype(jnp.bfloat16),
            v_ref[b, :r1, :],
            preferred_element_type=jnp.float32,
        )
        summed = (summed * jnp.where(live, 1.0 / totals, 0.0)).astype(jnp.bfloat16)
        for h in range(heads):
            out_ref[b, :, h * HEAD_SIZE : (h + 1) * HEAD_SIZE] = summed[h * rows : (h + 1) * rows]


def attend(q, k, v, ids, r0, r1):
    cols = q.shape[2]
    spec = lambda w: pl.BlockSpec((STEP_BLOCKS, BLOCK, w), lambda i: (i, 0, 0))
    return pl.pallas_call(
        lambda *refs: attend_kernel(r0, r1, *refs),
        grid=(NB // STEP_BLOCKS,),
        in_specs=[
            spec(cols),
            spec(k.shape[2]),
            spec(v.shape[2]),
            pl.BlockSpec((1, STEP_BLOCKS, BLOCK), lambda i: (i, 0, 0)),
        ],
        out_specs=pl.BlockSpec((STEP_BLOCKS, r1 - r0, cols), lambda i: (i, 0, 0)),
        out_shape=jax.ShapeDtypeStruct((NB, r1 - r0, cols), q.dtype),
        cost_estimate=pl.CostEstimate(
            flops=NB * 4 * (r1 - r0) * r1 * HEAD_SIZE * 4,
            bytes_accessed=8 * NB * BLOCK * cols,
            transcendentals=NB * 4 * (r1 - r0) * r1,
        ),
    )(q, k, v, ids.reshape(NB // STEP_BLOCKS, STEP_BLOCKS, BLOCK))


def next_label(low, residue, period):
    return low + rem(residue - low, period)


def send_kernel(f_ref, own_ref, other_ref, out_ref):
    me = f_ref[OWN]
    core = rem(me, NC)
    chip = me - core
    low, middle, high = f_ref[chip], f_ref[chip + 1], f_ref[chip + 2]
    for target in range(CHIPS):
        label = next_label(low, target * NC + core, DP)
        label = jnp.where(label < high, label, low)
        side = (label >= middle).astype(jnp.int32)
        block = label - jnp.where(side == 1, middle, low)
        out_ref[target] = jnp.where(side == core, own_ref[block], other_ref[block])


def place_kernel(f_ref, in_ref, out_ref):
    me = f_ref[OWN]
    for source in range(CHIPS):
        label = next_label(f_ref[source * NC], me, DP)

        @pl.when(label < f_ref[source * NC + NC])
        def _():
            out_ref[label // DP] = in_ref[source]


def weight_kernel(f_ref, *rest):
    pieces, out_ref = rest[:-1], rest[-1]
    me = f_ref[OWN]
    core = rem(me, NC)
    y = me // (NZ * NC)
    x = f_ref[MP]
    for t in range(NY):
        offset = rem(y - t - x, 4)
        place = jnp.where(offset == 3, 1, jnp.where(offset == 0, 0, offset + 1))
        out_ref[place, :, core] = pieces[t][...]
        out_ref[place, :, 1 - core] = pieces[NY + t][...]


ANY = pl.BlockSpec(memory_space=pl.ANY)
HBM = pl.BlockSpec(memory_space=pltpu.HBM)
VMEM = pl.BlockSpec(memory_space=pltpu.VMEM)
SMEM = pl.BlockSpec(memory_space=pltpu.SMEM)


def copies(kernel, shapes, firsts, *operands):
    shapes = [jax.ShapeDtypeStruct(s, jnp.bfloat16) for s in shapes]
    moved = sum(2 * 2 * math.prod(s.shape) for s in shapes)
    result = pl.pallas_call(
        kernel,
        in_specs=[SMEM] + [VMEM] * len(operands),
        out_specs=[VMEM] * len(shapes),
        out_shape=shapes,
        cost_estimate=pl.CostEstimate(flops=10**7, bytes_accessed=moved, transcendentals=0),
    )(firsts, *operands)
    return result


def project_kernel(halves, r0, *rest):
    mine, left, right = rest[:3]
    fars = rest[3 : 3 + halves]
    w_ref = rest[3 + halves]
    out_ref, y_ref, sem = rest[-3:]
    rows, depth = mine.shape[1:]
    width = w_ref.shape[-1]
    stores = []
    for step in range(KEPT // FIRST):
        first = step * FIRST
        far = fars[step][...] if halves == 2 else fars[0][first : first + FIRST]
        pieces = [ref[first : first + FIRST] for ref in (mine, left, right)] + [far]
        joined = jnp.concatenate([p.reshape(FIRST * rows, depth) for p in pieces], axis=1)
        for n in range(0, width, N_TILE):
            weight = w_ref[..., n : n + N_TILE].reshape(4 * depth, N_TILE)
            total = jnp.dot(joined, weight, preferred_element_type=jnp.float32)
            y_ref[first : first + FIRST, :, n : n + N_TILE] = total.astype(jnp.bfloat16).reshape(
                FIRST, rows, N_TILE
            )
        stores.append(
            pltpu.make_async_copy(
                y_ref.at[first : first + FIRST],
                out_ref.at[first : first + FIRST, r0 : r0 + rows],
                sem.at[step],
            )
        )
        stores[-1].start()
    for store in stores:
        store.wait()


def project(pieces, weight, r0, r1, out):
    rows, depth = r1 - r0, pieces[0].shape[2]
    width = weight.shape[-1]
    halves = len(pieces) - 3
    operands = [*pieces, weight]
    in_specs = [VMEM] * len(operands)
    aliases = {}
    if out is not None:
        in_specs.append(HBM)
        aliases = {len(operands): 0}
        operands.append(out)
    return pl.pallas_call(
        lambda *refs: project_kernel(halves, r0, *refs),
        in_specs=in_specs,
        out_specs=HBM,
        out_shape=jax.ShapeDtypeStruct((KEPT, BLOCK, width), jnp.bfloat16),
        scratch_shapes=[
            pltpu.VMEM((KEPT, rows, width), jnp.bfloat16),
            pltpu.SemaphoreType.DMA((KEPT // FIRST,)),
        ],
        input_output_aliases=aliases,
        cost_estimate=pl.CostEstimate(
            flops=2 * KEPT * rows * 4 * depth * width,
            bytes_accessed=2 * (KEPT * rows * (4 * depth + width) + 4 * depth * width),
            transcendentals=0,
        ),
    )(*operands)


def dp_pairs(dy=0, dz=0, swap=False):
    pairs = []
    for d in range(DP):
        y, z, c = d // (NZ * NC), d // NC % NZ, d % NC
        if swap:
            c = 1 - c
        pairs.append((d, ((y + dy) % NY * NZ + (z + dz) % NZ) * NC + c))
    return pairs


def ring(size, shift):
    return [(i, (i + shift) % size) for i in range(size)]


Z_GROUPS = [[(y * NZ + z) * NC + c for z in range(NZ)] for y in range(NY) for c in range(NC)]
CHIP_GROUPS = [[chip * NC + c for chip in range(CHIPS)] for c in range(NC)]


def step(queries, keys, values, doc_ids, live_counts, out_weight):
    own_index = lax.axis_index("dp")
    mp_index = lax.axis_index("mp")
    table = lax.all_to_all(
        jnp.broadcast_to(live_counts[None], (DP, 1)), "dp", 0, 0, tiled=True
    ).reshape(DP)
    places = jnp.arange(128, dtype=jnp.int32)
    firsts = jnp.sum(
        jnp.where(jnp.arange(DP, dtype=jnp.int32)[None, :] < places[:, None], table[None, :], 0),
        axis=1,
    )
    firsts = jnp.where(places == OWN, own_index, jnp.where(places == MP, mp_index, firsts))
    cols = queries.shape[1]
    q = queries.reshape(NB, BLOCK, cols)
    k = keys.reshape(NB, BLOCK, keys.shape[1])
    v = values.reshape(NB, BLOCK, values.shape[1])
    ids = doc_ids.reshape(NB, BLOCK)
    results = []
    share, width = out_weight.shape
    last = len(CHUNKS) - 1
    for n, (r0, r1) in enumerate(CHUNKS):
        rows = r1 - r0
        own = attend(q, k, v, ids, r0, r1)
        other = lax.ppermute(own, "dp", dp_pairs(swap=True))
        (z_out,) = copies(send_kernel, [(CHIPS, rows, cols)], firsts, own, other)
        if n == last:
            weight, _ = lax.optimization_barrier((out_weight, z_in))
            w_z = lax.all_to_all(
                jnp.broadcast_to(weight[None], (NZ, share, width)), "dp", 0, 0,
                tiled=True, axis_index_groups=Z_GROUPS,
            )
            z_out, w_z = lax.optimization_barrier((z_out, w_z))
        z_in = lax.all_to_all(z_out, "dp", 0, 0, tiled=True, axis_index_groups=CHIP_GROUPS)
        (mine,) = copies(place_kernel, [(KEPT, rows, cols)], firsts, z_in)
        left = lax.ppermute(mine, "mp", ring(4, 1))
        right = lax.ppermute(mine, "mp", ring(4, 3))
        if n == last:
            far_a = lax.ppermute(left[:FIRST], "mp", ring(4, 1))
            far_b = lax.ppermute(right[FIRST:], "mp", ring(4, 3))
            results.append((mine, left, right, far_a, far_b))
        else:
            far = lax.ppermute((left, right)[n % 2], "mp", ring(4, (1, 3)[n % 2]))
            results.append((mine, left, right, far))
    pieces = [w_z]
    for t in range(1, NY):
        pieces.append(lax.ppermute(w_z, "dp", dp_pairs(dy=t)))
    for t in range(NY):
        pieces.append(lax.ppermute(pieces[t], "dp", dp_pairs(swap=True)))
    (weight,) = copies(weight_kernel, [(4, NZ, NC, share, width)], firsts, *pieces)
    out = None
    for (r0, r1), pieces in zip(CHUNKS, results):
        out = project(pieces, weight, r0, r1, out)
    return out.reshape(KEPT * BLOCK, width)


def solution(mesh):
    return jax.shard_map(
        step,
        mesh=mesh,
        in_specs=(
            P("dp", "mp"), P("dp", "mp"), P("dp", "mp"), P("dp"), P("dp"), P("dp", "mp"),
        ),
        out_specs=P("dp", "mp"),
        check_vma=False,
    )
```

time: 427 us -> 291 us (0.68)
  waiting for transfers between devices: 307 us -> 142 us
  Pallas kernels: 0 us -> 71 us
  starting transfers between devices: 32.3 us -> 65.7 us
  matrix products: 32.6 us -> 0 us
  local copies, waits for them, and re-layouts: 28.3 us -> 7.5 us
  between operations: 14.1 us -> 1 us
  other arithmetic: 11.8 us -> 1.87 us
    all_to_all x3 -> x5, waiting for transfers between devices: 198 us -> 67.9 us  [the longest x3 58.6 us: step(): lax.all_to_all(z_out, 'dp', 0, 0, tiled=True, axis_index_groups=CHIP_GROUPS)]
    all_gather x2 -> x0, waiting for transfers between devices: 109 us -> none  [the longest x1 109 us: body(): lax.all_gather(flattened, 'mp', axis=1, tiled=True)]
    ppermute x0 -> x20, waiting for transfers between devices: none -> 74.4 us  [the longest x3 33.8 us: step(): left = lax.ppermute(mine, 'mp', ring(4, 1))]
    pallas_call x0 -> x13, Pallas kernels: none -> 71 us  [the longest x3 25.4 us: project(): pl.pallas_call(lambda *refs: project_kernel(halves, r0, *refs), in_specs=...]
    dot_general x13 -> x0, matrix products: 32.6 us -> none  [the longest x1 17.8 us: body(): jnp.dot(lax.all_gather(flattened, 'mp', axis=1, tiled=True), full_weight,...]
    ppermute x0 -> x20, starting transfers between devices: none -> 30.8 us  [the longest x3 6.68 us: step(): other = lax.ppermute(own, 'dp', dp_pairs(swap=True))]
    gather x2 -> x0, local copies, waits for them, and re-layouts: 13.1 us -> none  [the longest x1 7.33 us: body(): own_result[chosen]]
    dynamic_slice x12 -> x0, local copies, waits for them, and re-layouts: 8.21 us -> none  [attend_blocks(): lax.map(attend_group, (regroup(query_blocks), regroup(key_blocks), regrou...]
  transfers between devices with their start and end apart: 5 -> 25, of which waited for: 3 -> 10; matrix products, arithmetic and copies ran while one was open for 12% -> 1% of each run, Pallas kernels for 0% -> 18%
where the time goes in v1:
time: 291 us; the launch traced here: 289 us
  waiting for transfers between devices  142 us (49%)
  Pallas kernels  71 us (24%)
  starting transfers between devices  65.7 us (23%)
  local copies, waits for them, and re-layouts  7.5 us (3%)
    all_to_all x3, waiting for transfers between devices, step(): lax.all_to_all(z_out, 'dp', 0, 0, tiled=True, axis_index_groups=CHIP_GROUPS)  58.6 us
    ppermute x3, waiting for transfers between devices, step(): left = lax.ppermute(mine, 'mp', ring(4, 1))  33.8 us
    ppermute x3, waiting for transfers between devices, step(): right = lax.ppermute(mine, 'mp', ring(4, 3))  29.2 us
    pallas_call x3, Pallas kernels, project(): pl.pallas_call(lambda *refs: project_kernel(halves, r0, *refs), in_specs=...  25.4 us
    pallas_call x3, Pallas kernels, attend(): pl.pallas_call(lambda *refs: attend_kernel(r0, r1, *refs), grid=(NB // ST...  24.5 us
    pallas_call x7, Pallas kernels, copies(): pl.pallas_call(kernel, in_specs=[SMEM] + [VMEM] * len(operands), out_spec...  21.2 us
    all_to_all x3, starting transfers between devices, step(): lax.all_to_all(z_out, 'dp', 0, 0, tiled=True, axis_index_groups=CHIP_GROUPS)  20.3 us
    all_to_all x1, starting transfers between devices, step(): lax.all_to_all(jnp.broadcast_to(live_counts[None], (DP, 1)), 'dp', 0, 0,...  10.1 us
  transfers between devices with their start and end apart: 25, of which 10 were waited for; matrix products, arithmetic and copies ran while one was open for 1% of the time, Pallas kernels for 18%

profile of v1, /device:TPU:1, one launch (start us, length us, event | category | flops | bytes accessed | tf_op | source)
XLA Modules:
  0.0 289.4 jit_solution(13277110278492676598)
XLA Ops:
  0.0 7.6 %shard_map.66.own_ref = bf16[24,48,512]{2,1,0:T(8,128)(2,1)} custom-call(bf16[24,128,512]{2,1,0:T(8,128)(2,1)} %bitcast.7, bf16[24,128,128]{2,1,0:T(8,128)(2,1)} %bitcast.10, bf16[24,128,128]{2,1,0:T(8,128)(2,1)} %bitcast.13, s32[6,4,128]{2,1,0:T(4,128)} %bitcast.16), custom_call_target="tpu_custom_call" | custom-call | flops 226492416 | bytes 12582912 | tf_op jit(solution)/shard_map/pallas_call | solution.py:75
  7.6 3.2 %collective-permute-start.1 = (bf16[24,48,512]{2,1,0:T(8,128)(2,1)}, bf16[24,48,512]{2,1,0:T(8,128)(2,1)S(1)}, u32[]{:S(2)}, u32[]{:S(2)}) collective-permute-start(bf16[24,48,512]{2,1,0:T(8,128)(2,1)} %shard_map.66.own_ref), channel_id=1, source_target_pairs={{0,4},{4,0},{8,12},{12,8},{16,20},{20,16},{24,28},{28,24},{32,36},... | collective-permute-start | bytes 3538952 | tf_op jit(solution)/shard_map/ppermute | solution.py:254
  12.1 10.1 %all-to-all-start = ((s32[64,1,1]{2,1,0:T(1,128)}), s32[64,1,1]{2,1,0:T(1,128)S(1)}, u32[]{:S(2)}, u32[]{:S(2)}) async-start(s32[64,1,1]{2,1,0:T(1,128)} %broadcast_in_dim.40), calls=%async_computation | async-start | bytes 65536 | tf_op jit(solution)/shard_map/all_to_all | solution.py:234
  22.2 9.2 %all-to-all-done = s32[64,1,1]{2,1,0:T(1,128)S(1)} async-done(((s32[64,1,1]{2,1,0:T(1,128)}), s32[64,1,1]{2,1,0:T(1,128)S(1)}, u32[]{:S(2)}, u32[]{:S(2)}) %all-to-all-start) | async-done | bytes 288 | tf_op jit(solution)/shard_map/all_to_all | solution.py:234
  34.3 3.0 %shard_map.67 = bf16[32,48,512]{2,1,0:T(8,128)(2,1)} custom-call(s32[128]{0:T(128)} %compare_select_fusion.1.f_ref, bf16[24,48,512]{2,1,0:T(8,128)(2,1)} %shard_map.66.own_ref, bf16[24,48,512]{2,1,0:T(8,128)(2,1)} %copy-done.6), custom_call_target="tpu_custom_call" | custom-call | flops 10000000 | bytes 3145728 | tf_op jit(solution)/shard_map/pallas_call | solution.py:143
  37.3 4.0 %all-to-all-start.1 = ((bf16[32,48,512]{2,1,0:T(8,128)(2,1)}), bf16[32,48,512]{2,1,0:T(8,128)(2,1)S(1)}, u32[]{:S(2)}, u32[]{:S(2)}) async-start(bf16[32,48,512]{2,1,0:T(8,128)(2,1)} %shard_map.67), calls=%async_computation.1 | async-start | bytes 3145728 | tf_op jit(solution)/shard_map/all_to_all | solution.py:263
  41.3 7.5 %shard_map.71.own_ref = bf16[24,48,512]{2,1,0:T(8,128)(2,1)} custom-call(bf16[24,128,512]{2,1,0:T(8,128)(2,1)} %bitcast.8, bf16[24,128,128]{2,1,0:T(8,128)(2,1)} %bitcast.11, bf16[24,128,128]{2,1,0:T(8,128)(2,1)} %bitcast.14, s32[6,4,128]{2,1,0:T(4,128)} %bitcast.17), custom_call_target="tpu_custom_call" | custom-call | flops 113246208 | bytes 12582912 | tf_op jit(solution)/shard_map/pallas_call | solution.py:75
  53.2 3.0 %shard_map.72 = bf16[32,48,512]{2,1,0:T(8,128)(2,1)} custom-call(s32[128]{0:T(128)} %compare_select_fusion.1.f_ref, bf16[24,48,512]{2,1,0:T(8,128)(2,1)} %shard_map.71.own_ref, bf16[24,48,512]{2,1,0:T(8,128)(2,1)} %copy-done.7), custom_call_target="tpu_custom_call" | custom-call | flops 10000000 | bytes 3145728 | tf_op jit(solution)/shard_map/pallas_call | solution.py:143
  56.2 21.7 %all-to-all-done.1.in_ref = bf16[32,48,512]{2,1,0:T(8,128)(2,1)S(1)} async-done(((bf16[32,48,512]{2,1,0:T(8,128)(2,1)}), bf16[32,48,512]{2,1,0:T(8,128)(2,1)S(1)}, u32[]{:S(2)}, u32[]{:S(2)}) %all-to-all-start.1) | async-done | bytes 1572896 | tf_op jit(solution)/shard_map/all_to_all | solution.py:263
  79.0 7.8 %all-to-all-start.4 = ((bf16[32,48,512]{2,1,0:T(8,128)(2,1)}), bf16[32,48,512]{2,1,0:T(8,128)(2,1)S(1)}, u32[]{:S(2)}, u32[]{:S(2)}) async-start(bf16[32,48,512]{2,1,0:T(8,128)(2,1)} %shard_map.72), calls=%async_computation.4 | async-start | bytes 3145728 | tf_op jit(solution)/shard_map/all_to_all | solution.py:263
  86.8 36.9 %all-to-all-done.4.in_ref = bf16[32,48,512]{2,1,0:T(8,128)(2,1)S(1)} async-done(((bf16[32,48,512]{2,1,0:T(8,128)(2,1)}), bf16[32,48,512]{2,1,0:T(8,128)(2,1)S(1)}, u32[]{:S(2)}, u32[]{:S(2)}) %all-to-all-start.4) | async-done | bytes 1572896 | tf_op jit(solution)/shard_map/all_to_all | solution.py:263
  124.7 4.5 %all-to-all-start.2 = ((bf16[8,32,1024]{2,1,0:T(8,128)(2,1)}), bf16[8,32,1024]{2,1,0:T(8,128)(2,1)S(1)}, u32[]{:S(2)}, u32[]{:S(2)}) async-start(bf16[8,32,1024]{2,1,0:T(8,128)(2,1)} %broadcast_in_dim.44), calls=%async_computation.2 | async-start | bytes 1048576 | tf_op jit(solution)/shard_map/all_to_all | solution.py:258
  129.3 9.3 %shard_map.64.own_ref = bf16[24,32,512]{2,1,0:T(8,128)(2,1)} custom-call(bf16[24,128,512]{2,1,0:T(8,128)(2,1)} %bitcast.9, bf16[24,128,128]{2,1,0:T(8,128)(2,1)} %bitcast.12, bf16[24,128,128]{2,1,0:T(8,128)(2,1)} %bitcast.15, s32[6,4,128]{2,1,0:T(4,128)} %bitcast.18), custom_call_target="tpu_custom_call" | custom-call | flops 201326592 | bytes 12582912 | tf_op jit(solution)/shard_map/pallas_call | solution.py:75
  148.9 8.5 %all-to-all-start.3 = ((bf16[32,32,512]{2,1,0:T(8,128)(2,1)}), bf16[32,32,512]{2,1,0:T(8,128)(2,1)S(1)}, u32[]{:S(2)}, u32[]{:S(2)}) async-start(bf16[32,32,512]{2,1,0:T(8,128)(2,1)} %shard_map.65), calls=%async_computation.3 | async-start | bytes 2097152 | tf_op jit(solution)/shard_map/all_to_all | solution.py:263
  166.8 4.4 %collective-permute-done.17.refs_1_ = bf16[22,48,512]{2,1,0:T(8,128)(2,1)} collective-permute-done((bf16[22,48,512]{2,1,0:T(8,128)(2,1)}, bf16[22,48,512]{2,1,0:T(8,128)(2,1)}, u32[]{:S(2)}, u32[]{:S(2)}) %collective-permute-start.17) | collective-permute-done | bytes 1081376 | tf_op jit(solution)/shard_map/ppermute | solution.py:265
  172.1 10.6 %collective-permute-done.18.refs_2_ = bf16[22,48,512]{2,1,0:T(8,128)(2,1)} collective-permute-done((bf16[22,48,512]{2,1,0:T(8,128)(2,1)}, bf16[22,48,512]{2,1,0:T(8,128)(2,1)}, u32[]{:S(2)}, u32[]{:S(2)}) %collective-permute-start.18) | collective-permute-done | bytes 1081376 | tf_op jit(solution)/shard_map/ppermute | solution.py:266
  187.1 18.6 %collective-permute-done.14.refs_2_ = bf16[22,48,512]{2,1,0:T(8,128)(2,1)S(1)} collective-permute-done((bf16[22,48,512]{2,1,0:T(8,128)(2,1)}, bf16[22,48,512]{2,1,0:T(8,128)(2,1)S(1)}, u32[]{:S(2)}, u32[]{:S(2)}) %collective-permute-start.14) | collective-permute-done | bytes 1081376 | tf_op jit(solution)/shard_map/ppermute | solution.py:266
  218.4 4.4 %shard_map.69.refs_4_.refs_5_ = bf16[4,8,2,32,1024]{4,3,2,1,0:T(8,128)(2,1)} custom-call(s32[128]{0:T(128)} %compare_select_fusion.1.f_ref, bf16[8,32,1024]{2,1,0:T(8,128)(2,1)} %copy-done.3, bf16[8,32,1024]{2,1,0:T(8,128)(2,1)} %copy-done.10, bf16[8,32,1024]{2,1,0:T(8,128)(2,1)} %collective-permute-done.7.rest_2_, ...), custom_call_target="tpu_custom_call" | custom-call | flops 10000000 | bytes 8388608 | tf_op jit(solution)/shard_map/pallas_call | solution.py:143
  222.8 8.4 %collective-permute-done.19.refs_3_ = bf16[22,48,512]{2,1,0:T(8,128)(2,1)} collective-permute-done((bf16[22,48,512]{2,1,0:T(8,128)(2,1)}, bf16[22,48,512]{2,1,0:T(8,128)(2,1)}, u32[]{:S(2)}, u32[]{:S(2)}) %collective-permute-start.19) | collective-permute-done | bytes 1081376 | tf_op jit(solution)/shard_map/ppermute | solution.py:272
  231.3 9.1 %shard_map.74.refs_5_ = bf16[22,128,1024]{2,1,0:T(8,128)(2,1)} custom-call(bf16[22,48,512]{2,1,0:T(8,128)(2,1)} %shard_map.73.refs_0_, bf16[22,48,512]{2,1,0:T(8,128)(2,1)} %collective-permute-done.17.refs_1_, bf16[22,48,512]{2,1,0:T(8,128)(2,1)} %collective-permute-done.18.refs_2_, bf16[22,48,512]{2,1,0:T(8,128)(2,1)} %collective-permute-done.19.refs_3_, ...), custom_call_target="tpu_custom_call" | custom-call | flops 4429185024 | bytes 10682368 | tf_op jit(solution)/shard_map/pallas_call | solution.py:195
  240.4 29.4 %collective-permute-done.2.refs_1_ = bf16[22,32,512]{2,1,0:T(8,128)(2,1)S(1)} collective-permute-done((bf16[22,32,512]{2,1,0:T(8,128)(2,1)}, bf16[22,32,512]{2,1,0:T(8,128)(2,1)S(1)}, u32[]{:S(2)}, u32[]{:S(2)}) %collective-permute-start.2) | collective-permute-done | bytes 720928 | tf_op jit(solution)/shard_map/ppermute | solution.py:265
  270.0 2.9 %collective-permute-start.5 = (bf16[11,32,512]{2,1,0:T(8,128)(2,1)S(1)}, bf16[11,32,512]{2,1,0:T(8,128)(2,1)}, u32[]{:S(2)}, u32[]{:S(2)}) collective-permute-start(bf16[11,32,512]{2,1,0:T(8,128)(2,1)S(1)} %slice.9), channel_id=1, source_target_pairs={{0,3},{1,0},{2,1},{3,2},{4,7},{5,4},{6,5},{7,6},{8,11},{9,8},{10,9... | collective-permute-start | bytes 1081352 | tf_op jit(solution)/shard_map/ppermute | solution.py:269
  272.9 9.1 %shard_map.75.refs_6_ = bf16[22,128,1024]{2,1,0:T(8,128)(2,1)} custom-call(bf16[22,48,512]{2,1,0:T(8,128)(2,1)} %shard_map.70.refs_0_, bf16[22,48,512]{2,1,0:T(8,128)(2,1)} %collective-permute-done.13.refs_1_, bf16[22,48,512]{2,1,0:T(8,128)(2,1)} %copy-done.8, bf16[22,48,512]{2,1,0:T(8,128)(2,1)} %collective-permute-done.15.refs_3_, ...), custom_call_target="tpu_custom_call", output_to_operand_aliasing={{}: (5, {})} | custom-call | flops 4429185024 | bytes 10682368 | tf_op jit(solution)/shard_map/pallas_call | solution.py:195
  282.1 7.1 %shard_map.76 = bf16[22,128,1024]{2,1,0:T(8,128)(2,1)} custom-call(bf16[22,32,512]{2,1,0:T(8,128)(2,1)} %shard_map.68.refs_0_, bf16[22,32,512]{2,1,0:T(8,128)(2,1)} %copy-done.4, bf16[22,32,512]{2,1,0:T(8,128)(2,1)} %copy-done.5, bf16[11,32,512]{2,1,0:T(8,128)(2,1)} %collective-permute-done.4.refs_3_, ...), custom_call_target="tpu_custom_call", output_to_operand_aliasing={{}: (6, {})} | custom-call | flops 2952790016 | bytes 8519680 | tf_op jit(solution)/shard_map/pallas_call | solution.py:195
  (74 shorter events, 47.8 us)
Async XLA Ops:
  7.6 25.7 %collective-permute-start.1 = (bf16[24,48,512]{2,1,0:T(8,128)(2,1)}, bf16[24,48,512]{2,1,0:T(8,128)(2,1)S(1)}, u32[]{:S(2)}, u32[]{:S(2)}) collective-permute-start(bf16[24,48,512]{2,1,0:T(8,128)(2,1)} %shard_map.66.own_ref), channel_id=1, source_target_pairs={{0,4},{4,0},{8,12},{12,8},{16,20},{20,16},{24,28},{28,24},{32,36},... | collective-permute-start | bytes 3538952 | tf_op jit(solution)/shard_map/ppermute | solution.py:254
  12.1 19.3 %all-to-all-start = ((s32[64,1,1]{2,1,0:T(1,128)}), s32[64,1,1]{2,1,0:T(1,128)S(1)}, u32[]{:S(2)}, u32[]{:S(2)}) async-start(s32[64,1,1]{2,1,0:T(1,128)} %broadcast_in_dim.40), calls=%async_computation | async-start | bytes 65536 | tf_op jit(solution)/shard_map/all_to_all | solution.py:234
  37.3 40.6 %all-to-all-start.1 = ((bf16[32,48,512]{2,1,0:T(8,128)(2,1)}), bf16[32,48,512]{2,1,0:T(8,128)(2,1)S(1)}, u32[]{:S(2)}, u32[]{:S(2)}) async-start(bf16[32,48,512]{2,1,0:T(8,128)(2,1)} %shard_map.67), calls=%async_computation.1 | async-start | bytes 3145728 | tf_op jit(solution)/shard_map/all_to_all | solution.py:263
  79.0 44.8 %all-to-all-start.4 = ((bf16[32,48,512]{2,1,0:T(8,128)(2,1)}), bf16[32,48,512]{2,1,0:T(8,128)(2,1)S(1)}, u32[]{:S(2)}, u32[]{:S(2)}) async-start(bf16[32,48,512]{2,1,0:T(8,128)(2,1)} %shard_map.72), calls=%async_computation.4 | async-start | bytes 3145728 | tf_op jit(solution)/shard_map/all_to_all | solution.py:263
  124.7 24.2 %all-to-all-start.2 = ((bf16[8,32,1024]{2,1,0:T(8,128)(2,1)}), bf16[8,32,1024]{2,1,0:T(8,128)(2,1)S(1)}, u32[]{:S(2)}, u32[]{:S(2)}) async-start(bf16[8,32,1024]{2,1,0:T(8,128)(2,1)} %broadcast_in_dim.44), calls=%async_computation.2 | async-start | bytes 1048576 | tf_op jit(solution)/shard_map/all_to_all | solution.py:258
  138.6 6.9 %collective-permute-start = (bf16[24,32,512]{2,1,0:T(8,128)(2,1)}, bf16[24,32,512]{2,1,0:T(8,128)(2,1)S(1)}, u32[]{:S(2)}, u32[]{:S(2)}) collective-permute-start(bf16[24,32,512]{2,1,0:T(8,128)(2,1)} %shard_map.64.own_ref), channel_id=1, source_target_pairs={{0,4},{4,0},{8,12},{12,8},{16,20},{20,16},{24,28},{28,24},{32,36},... | collective-permute-start | bytes 2359304 | tf_op jit(solution)/shard_map/ppermute | solution.py:254
  144.3 26.9 %collective-permute-start.17 = (bf16[22,48,512]{2,1,0:T(8,128)(2,1)}, bf16[22,48,512]{2,1,0:T(8,128)(2,1)}, u32[]{:S(2)}, u32[]{:S(2)}) collective-permute-start(bf16[22,48,512]{2,1,0:T(8,128)(2,1)} %shard_map.73.refs_0_), channel_id=1, source_target_pairs={{0,1},{1,2},{2,3},{3,0},{4,5},{5,6},{6,7},{7,4},{8,9},{9,10},{10,1... | collective-permute-start | bytes 3244040 | tf_op jit(solution)/shard_map/ppermute | solution.py:265
  148.9 63.3 %all-to-all-start.3 = ((bf16[32,32,512]{2,1,0:T(8,128)(2,1)}), bf16[32,32,512]{2,1,0:T(8,128)(2,1)S(1)}, u32[]{:S(2)}, u32[]{:S(2)}) async-start(bf16[32,32,512]{2,1,0:T(8,128)(2,1)} %shard_map.65), calls=%async_computation.3 | async-start | bytes 2097152 | tf_op jit(solution)/shard_map/all_to_all | solution.py:263
  157.4 25.2 %collective-permute-start.18 = (bf16[22,48,512]{2,1,0:T(8,128)(2,1)}, bf16[22,48,512]{2,1,0:T(8,128)(2,1)}, u32[]{:S(2)}, u32[]{:S(2)}) collective-permute-start(bf16[22,48,512]{2,1,0:T(8,128)(2,1)} %shard_map.73.refs_0_), channel_id=1, source_target_pairs={{0,3},{1,0},{2,1},{3,2},{4,7},{5,4},{6,5},{7,6},{8,11},{9,8},{10,9... | collective-permute-start | bytes 3244040 | tf_op jit(solution)/shard_map/ppermute | solution.py:266
  161.9 43.9 %collective-permute-start.14 = (bf16[22,48,512]{2,1,0:T(8,128)(2,1)}, bf16[22,48,512]{2,1,0:T(8,128)(2,1)S(1)}, u32[]{:S(2)}, u32[]{:S(2)}) collective-permute-start(bf16[22,48,512]{2,1,0:T(8,128)(2,1)} %shard_map.70.refs_0_), channel_id=1, source_target_pairs={{0,3},{1,0},{2,1},{3,2},{4,7},{5,4},{6,5},{7,6},{8,11},{9,8},{10,9... | collective-permute-start | bytes 3244040 | tf_op jit(solution)/shard_map/ppermute | solution.py:266
  163.1 22.3 %collective-permute-start.6 = (bf16[8,32,1024]{2,1,0:T(8,128)(2,1)S(1)}, bf16[8,32,1024]{2,1,0:T(8,128)(2,1)S(1)}, u32[]{:S(2)}, u32[]{:S(2)}) collective-permute-start(bf16[8,32,1024]{2,1,0:T(8,128)(2,1)S(1)} %all-to-all-done.2.rest_0_), channel_id=1, source_target_pairs={{0,64},{4,68},{8,72},{12,76},{16,80},{20,84},{24,88},{28,92},{32,9... | collective-permute-start | bytes 1572872 | tf_op jit(solution)/shard_map/ppermute | solution.py:276
  164.4 42.6 %collective-permute-start.7 = (bf16[8,32,1024]{2,1,0:T(8,128)(2,1)S(1)}, bf16[8,32,1024]{2,1,0:T(8,128)(2,1)}, u32[]{:S(2)}, u32[]{:S(2)}) collective-permute-start(bf16[8,32,1024]{2,1,0:T(8,128)(2,1)S(1)} %all-to-all-done.2.rest_0_), channel_id=1, source_target_pairs={{0,128},{4,132},{8,136},{12,140},{16,144},{20,148},{24,152},{28,15... | collective-permute-start | bytes 1572872 | tf_op jit(solution)/shard_map/ppermute | solution.py:276
  171.2 37.4 %collective-permute-start.8 = (bf16[8,32,1024]{2,1,0:T(8,128)(2,1)S(1)}, bf16[8,32,1024]{2,1,0:T(8,128)(2,1)}, u32[]{:S(2)}, u32[]{:S(2)}) collective-permute-start(bf16[8,32,1024]{2,1,0:T(8,128)(2,1)S(1)} %all-to-all-done.2.rest_0_), channel_id=1, source_target_pairs={{0,192},{4,196},{8,200},{12,204},{16,208},{20,212},{24,216},{28,22... | collective-permute-start | bytes 1572872 | tf_op jit(solution)/shard_map/ppermute | solution.py:276
  182.7 26.1 %collective-permute-start.9 = (bf16[8,32,1024]{2,1,0:T(8,128)(2,1)S(1)}, bf16[8,32,1024]{2,1,0:T(8,128)(2,1)S(1)}, u32[]{:S(2)}, u32[]{:S(2)}) collective-permute-start(bf16[8,32,1024]{2,1,0:T(8,128)(2,1)S(1)} %all-to-all-done.2.rest_0_), channel_id=1, source_target_pairs={{0,4},{4,0},{8,12},{12,8},{16,20},{20,16},{24,28},{28,24},{32,36},... | collective-permute-start | bytes 1572872 | tf_op jit(solution)/shard_map/ppermute | solution.py:278
  185.4 24.3 %collective-permute-start.10 = (bf16[8,32,1024]{2,1,0:T(8,128)(2,1)S(1)}, bf16[8,32,1024]{2,1,0:T(8,128)(2,1)S(1)}, u32[]{:S(2)}, u32[]{:S(2)}) collective-permute-start(bf16[8,32,1024]{2,1,0:T(8,128)(2,1)S(1)} %collective-permute-done.6.rest_1_), channel_id=1, source_target_pairs={{0,4},{4,0},{8,12},{12,8},{16,20},{20,16},{24,28},{28,24},{32,36},... | collective-permute-start | bytes 1572872 | tf_op jit(solution)/shard_map/ppermute | solution.py:278
  205.7 25.5 %collective-permute-start.19 = (bf16[22,48,512]{2,1,0:T(8,128)(2,1)}, bf16[22,48,512]{2,1,0:T(8,128)(2,1)}, u32[]{:S(2)}, u32[]{:S(2)}) collective-permute-start(bf16[22,48,512]{2,1,0:T(8,128)(2,1)} %collective-permute-done.17.refs_1_), channel_id=1, source_target_pairs={{0,1},{1,2},{2,3},{3,0},{4,5},{5,6},{6,7},{7,4},{8,9},{9,10},{10,1... | collective-permute-start | bytes 3244040 | tf_op jit(solution)/shard_map/ppermute | solution.py:272
  207.0 8.8 %collective-permute-start.11 = (bf16[8,32,1024]{2,1,0:T(8,128)(2,1)}, bf16[8,32,1024]{2,1,0:T(8,128)(2,1)}, u32[]{:S(2)}, u32[]{:S(2)}) collective-permute-start(bf16[8,32,1024]{2,1,0:T(8,128)(2,1)} %collective-permute-done.7.rest_2_), channel_id=1, source_target_pairs={{0,4},{4,0},{8,12},{12,8},{16,20},{20,16},{24,28},{28,24},{32,36},... | collective-permute-start | bytes 1572872 | tf_op jit(solution)/shard_map/ppermute | solution.py:278
  208.7 7.1 %collective-permute-start.12 = (bf16[8,32,1024]{2,1,0:T(8,128)(2,1)}, bf16[8,32,1024]{2,1,0:T(8,128)(2,1)}, u32[]{:S(2)}, u32[]{:S(2)}) collective-permute-start(bf16[8,32,1024]{2,1,0:T(8,128)(2,1)} %collective-permute-done.8.rest_3_), channel_id=1, source_target_pairs={{0,4},{4,0},{8,12},{12,8},{16,20},{20,16},{24,28},{28,24},{32,36},... | collective-permute-start | bytes 1572872 | tf_op jit(solution)/shard_map/ppermute | solution.py:278
  208.8 64.1 %collective-permute-start.13 = (bf16[22,48,512]{2,1,0:T(8,128)(2,1)}, bf16[22,48,512]{2,1,0:T(8,128)(2,1)}, u32[]{:S(2)}, u32[]{:S(2)}) collective-permute-start(bf16[22,48,512]{2,1,0:T(8,128)(2,1)} %shard_map.70.refs_0_), channel_id=1, source_target_pairs={{0,1},{1,2},{2,3},{3,0},{4,5},{5,6},{6,7},{7,4},{8,9},{9,10},{10,1... | collective-permute-start | bytes 3244040 | tf_op jit(solution)/shard_map/ppermute | solution.py:265
  210.5 62.4 %collective-permute-start.15 = (bf16[22,48,512]{2,1,0:T(8,128)(2,1)S(1)}, bf16[22,48,512]{2,1,0:T(8,128)(2,1)}, u32[]{:S(2)}, u32[]{:S(2)}) collective-permute-start(bf16[22,48,512]{2,1,0:T(8,128)(2,1)S(1)} %collective-permute-done.14.refs_2_), channel_id=1, source_target_pairs={{0,3},{1,0},{2,1},{3,2},{4,7},{5,4},{6,5},{7,6},{8,11},{9,8},{10,9... | collective-permute-start | bytes 3244040 | tf_op jit(solution)/shard_map/ppermute | solution.py:272
  215.7 54.0 %collective-permute-start.2 = (bf16[22,32,512]{2,1,0:T(8,128)(2,1)}, bf16[22,32,512]{2,1,0:T(8,128)(2,1)S(1)}, u32[]{:S(2)}, u32[]{:S(2)}) collective-permute-start(bf16[22,32,512]{2,1,0:T(8,128)(2,1)} %shard_map.68.refs_0_), channel_id=1, source_target_pairs={{0,1},{1,2},{2,3},{3,0},{4,5},{5,6},{6,7},{7,4},{8,9},{9,10},{10,1... | collective-permute-start | bytes 2162696 | tf_op jit(solution)/shard_map/ppermute | solution.py:265
  215.8 54.1 %collective-permute-start.3 = (bf16[22,32,512]{2,1,0:T(8,128)(2,1)}, bf16[22,32,512]{2,1,0:T(8,128)(2,1)S(1)}, u32[]{:S(2)}, u32[]{:S(2)}) collective-permute-start(bf16[22,32,512]{2,1,0:T(8,128)(2,1)} %shard_map.68.refs_0_), channel_id=1, source_target_pairs={{0,3},{1,0},{2,1},{3,2},{4,7},{5,4},{6,5},{7,6},{8,11},{9,8},{10,9... | collective-permute-start | bytes 2162696 | tf_op jit(solution)/shard_map/ppermute | solution.py:266
  269.8 12.3 %collective-permute-start.4 = (bf16[11,32,512]{2,1,0:T(8,128)(2,1)S(1)}, bf16[11,32,512]{2,1,0:T(8,128)(2,1)}, u32[]{:S(2)}, u32[]{:S(2)}) collective-permute-start(bf16[11,32,512]{2,1,0:T(8,128)(2,1)S(1)} %slice.8), channel_id=1, source_target_pairs={{0,1},{1,2},{2,3},{3,0},{4,5},{5,6},{6,7},{7,4},{8,9},{9,10},{10,1... | collective-permute-start | bytes 1081352 | tf_op jit(solution)/shard_map/ppermute | solution.py:268
  270.0 12.1 %collective-permute-start.5 = (bf16[11,32,512]{2,1,0:T(8,128)(2,1)S(1)}, bf16[11,32,512]{2,1,0:T(8,128)(2,1)}, u32[]{:S(2)}, u32[]{:S(2)}) collective-permute-start(bf16[11,32,512]{2,1,0:T(8,128)(2,1)S(1)} %slice.9), channel_id=1, source_target_pairs={{0,3},{1,0},{2,1},{3,2},{4,7},{5,4},{6,5},{7,6},{8,11},{9,8},{10,9... | collective-permute-start | bytes 1081352 | tf_op jit(solution)/shard_map/ppermute | solution.py:269
  (15 other events, 200.8 us)

commit v2 on v1

--- a/solution.py
+++ b/solution.py
@@ -17,10 +17,13 @@
 NC = 2
 DP = NY * NZ * NC
 CHIPS = NY * NZ
+Z_SLOTS = 3
+Y_SLOTS = 6
 FIRST = 11
 N_TILE = 256
 STEP_BLOCKS = 4
 CHUNKS = ((0, 48), (48, 96), (96, 128))
+DIRECT = ()
 OWN = 100
 MP = 101
 masked_score = -1e30
@@ -30,69 +33,153 @@
     return jnp.bitwise_and(a, n - 1)
 
 
-def attend_kernel(r0, r1, q_ref, k_ref, v_ref, ids_ref, out_ref):
+def attend_kernel(r0, r1, q_hbm, k_hbm, v_hbm, ids_ref, out_ref, q_ref, k_ref, v_ref, sems):
     rows = r1 - r0
     heads = q_ref.shape[2] // HEAD_SIZE
-    ids = ids_ref[0]
-    ids_columns = jnp.transpose(ids)
     place_row = lax.broadcasted_iota(jnp.int32, (rows, r1), 0) + r0
     place_col = lax.broadcasted_iota(jnp.int32, (rows, r1), 1)
     causal = place_col <= place_row
     scale = math.log2(math.e) / math.sqrt(HEAD_SIZE)
-    for b in range(STEP_BLOCKS):
-        column = ids_columns[r0:r1, b : b + 1]
-        allowed = (column == ids[b : b + 1, :r1]) & causal
-        bias = jnp.where(allowed, 0.0, masked_score)
-        bias = jnp.concatenate([bias] * heads, axis=0)
-        live = jnp.concatenate([column] * heads, axis=0) >= 0
-        q = q_ref[b, r0:r1, :]
-        stacked = jnp.concatenate(
-            [q[:, h * HEAD_SIZE : (h + 1) * HEAD_SIZE] for h in range(heads)], axis=0
-        )
-        scores = lax.dot_general(
-            stacked,
-            k_ref[b, :r1, :],
-            (((1,), (1,)), ((), ())),
-            preferred_element_type=jnp.float32,
-        )
-        scores = scores * scale + bias
-        highest = jnp.max(scores, axis=1, keepdims=True)
-        weights = jnp.exp2(scores - highest)
-        totals = jnp.sum(weights, axis=1, keepdims=True)
-        summed = jnp.dot(
-            weights.astype(jnp.bfloat16),
-            v_ref[b, :r1, :],
-            preferred_element_type=jnp.float32,
-        )
-        summed = (summed * jnp.where(live, 1.0 / totals, 0.0)).astype(jnp.bfloat16)
-        for h in range(heads):
-            out_ref[b, :, h * HEAD_SIZE : (h + 1) * HEAD_SIZE] = summed[h * rows : (h + 1) * rows]
+
+    def loads(group):
+        blocks = pl.ds(group * STEP_BLOCKS, STEP_BLOCKS)
+        return [
+            pltpu.make_async_copy(
+                q_hbm.at[blocks, r0:r1], q_ref.at[blocks], sems.at[group, 0]
+            ),
+            pltpu.make_async_copy(
+                k_hbm.at[blocks, 0:r1], k_ref.at[blocks], sems.at[group, 1]
+            ),
+            pltpu.make_async_copy(
+                v_hbm.at[blocks, 0:r1], v_ref.at[blocks], sems.at[group, 2]
+            ),
+        ]
+
+    for group in range(NB // STEP_BLOCKS):
+        for load in loads(group):
+            load.start()
+
+    def some_blocks(group, carry):
+        for load in loads(group):
+            load.wait()
+        ids = ids_ref[group]
+        ids_columns = jnp.transpose(ids)
+        for b in range(STEP_BLOCKS):
+            block = group * STEP_BLOCKS + b
+            column = ids_columns[r0:r1, b : b + 1]
+            allowed = (column == ids[b : b + 1, :r1]) & causal
+            bias = jnp.where(allowed, 0.0, masked_score)
+            bias = jnp.concatenate([bias] * heads, axis=0)
+            live = jnp.concatenate([column] * heads, axis=0) >= 0
+            q = q_ref[block]
+            stacked = jnp.concatenate(
+                [q[:, h * HEAD_SIZE : (h + 1) * HEAD_SIZE] for h in range(heads)], axis=0
+            )
+            scores = lax.dot_general(
+                stacked,
+                k_ref[block],
+                (((1,), (1,)), ((), ())),
+                preferred_element_type=jnp.float32,
+            )
+            scores = scores * scale + bias
+            highest = jnp.max(scores, axis=1, keepdims=True)
+            weights = jnp.exp2(scores - highest)
+            totals = jnp.sum(weights, axis=1, keepdims=True)
+            summed = jnp.dot(
+                weights.astype(jnp.bfloat16),
+                v_ref[block],
+                preferred_element_type=jnp.float32,
+            )
+            summed = (summed * jnp.where(live, 1.0 / totals, 0.0)).astype(jnp.bfloat16)
+            for h in range(heads):
+                out_ref[block, :, h * HEAD_SIZE : (h + 1) * HEAD_SIZE] = summed[
+                    h * rows : (h + 1) * rows
+                ]
+        return carry
+
+    lax.fori_loop(0, NB // STEP_BLOCKS, some_blocks, 0)
 
 
 def attend(q, k, v, ids, r0, r1):
     cols = q.shape[2]
-    spec = lambda w: pl.BlockSpec((STEP_BLOCKS, BLOCK, w), lambda i: (i, 0, 0))
+    groups = NB // STEP_BLOCKS
     return pl.pallas_call(
         lambda *refs: attend_kernel(r0, r1, *refs),
-        grid=(NB // STEP_BLOCKS,),
-        in_specs=[
-            spec(cols),
-            spec(k.shape[2]),
-            spec(v.shape[2]),
-            pl.BlockSpec((1, STEP_BLOCKS, BLOCK), lambda i: (i, 0, 0)),
+        in_specs=[HBM, HBM, HBM, VMEM],
+        out_specs=VMEM,
+        out_shape=jax.ShapeDtypeStruct((NB, r1 - r0, cols), q.dtype),
+        scratch_shapes=[
+            pltpu.VMEM((NB, r1 - r0, cols), q.dtype),
+            pltpu.VMEM((NB, r1, k.shape[2]), k.dtype),
+            pltpu.VMEM((NB, r1, v.shape[2]), v.dtype),
+            pltpu.SemaphoreType.DMA((groups, 3)),
         ],
-        out_specs=pl.BlockSpec((STEP_BLOCKS, r1 - r0, cols), lambda i: (i, 0, 0)),
-        out_shape=jax.ShapeDtypeStruct((NB, r1 - r0, cols), q.dtype),
         cost_estimate=pl.CostEstimate(
             flops=NB * 4 * (r1 - r0) * r1 * HEAD_SIZE * 4,
             bytes_accessed=8 * NB * BLOCK * cols,
             transcendentals=NB * 4 * (r1 - r0) * r1,
         ),
-    )(q, k, v, ids.reshape(NB // STEP_BLOCKS, STEP_BLOCKS, BLOCK))
+        compiler_params=pltpu.CompilerParams(vmem_limit_bytes=60 << 20),
+    )(q, k, v, ids.reshape(groups, STEP_BLOCKS, BLOCK))
 
 
 def next_label(low, residue, period):
     return low + rem(residue - low, period)
+
+
+def to_z_kernel(f_ref, own_ref, other_ref, out_ref):
+    me = f_ref[OWN]
+    core = rem(me, NC)
+    chip = me - core
+    low, middle, high = f_ref[chip], f_ref[chip + 1], f_ref[chip + 2]
+    for z in range(NZ):
+        first = next_label(low, z * NC + core, NZ * NC)
+        for i in range(Z_SLOTS):
+            label = first + NZ * NC * i
+            label = jnp.where(label < high, label, low)
+            side = (label >= middle).astype(jnp.int32)
+            block = label - jnp.where(side == 1, middle, low)
+            out_ref[z * Z_SLOTS + i] = jnp.where(
+                side == core, own_ref[block], other_ref[block]
+            )
+
+
+def to_y_kernel(f_ref, in_ref, *rest):
+    outs = rest[:NY]
+    me = f_ref[OWN]
+    y = me // (NZ * NC)
+    within = rem(me, NZ * NC)
+    row = y * (NZ * NC)
+    low, high = f_ref[row], f_ref[row + NZ * NC]
+    for t in range(NY):
+        target = rem(y + t, NY) * (NZ * NC) + within
+        first = next_label(low, target, DP)
+        for i in range(Y_SLOTS):
+            label = first + DP * i
+            label = jnp.where(label < high, label, next_label(low, within, NZ * NC))
+            chip = jnp.int32(0)
+            for z in range(1, NZ):
+                chip = chip + (f_ref[row + z * NC] <= label).astype(jnp.int32)
+            start = next_label(f_ref[row + chip * NC], within, NZ * NC)
+            slot = chip * Z_SLOTS + (label - start) // (NZ * NC)
+            slot = jnp.clip(slot, 0, NZ * Z_SLOTS - 1)
+            outs[t][i] = in_ref[slot]
+
+
+def place_kernel(f_ref, *rest):
+    ins, out_ref = rest[:NY], rest[NY]
+    me = f_ref[OWN]
+    y = me // (NZ * NC)
+    for t in range(NY):
+        row = rem(y - t, NY) * (NZ * NC)
+        first = next_label(f_ref[row], me, DP)
+        high = f_ref[row + NZ * NC]
+        for i in range(Y_SLOTS):
+            label = first + DP * i
+
+            @pl.when(label < high)
+            def _():
+                out_ref[label // DP] = ins[t][i]
 
 
 def send_kernel(f_ref, own_ref, other_ref, out_ref):
@@ -108,7 +195,7 @@
         out_ref[target] = jnp.where(side == core, own_ref[block], other_ref[block])
 
 
-def place_kernel(f_ref, in_ref, out_ref):
+def receive_kernel(f_ref, in_ref, out_ref):
     me = f_ref[OWN]
     for source in range(CHIPS):
         label = next_label(f_ref[source * NC], me, DP)
@@ -146,6 +233,7 @@
         out_specs=[VMEM] * len(shapes),
         out_shape=shapes,
         cost_estimate=pl.CostEstimate(flops=10**7, bytes_accessed=moved, transcendentals=0),
+        compiler_params=pltpu.CompilerParams(vmem_limit_bytes=16 << 20),
     )(firsts, *operands)
     return result
 
@@ -207,6 +295,7 @@
             bytes_accessed=2 * (KEPT * rows * (4 * depth + width) + 4 * depth * width),
             transcendentals=0,
         ),
+        compiler_params=pltpu.CompilerParams(vmem_limit_bytes=32 << 20),
     )(*operands)
 
 
@@ -225,6 +314,7 @@
 
 
 Z_GROUPS = [[(y * NZ + z) * NC + c for z in range(NZ)] for y in range(NY) for c in range(NC)]
+
 CHIP_GROUPS = [[chip * NC + c for chip in range(CHIPS)] for c in range(NC)]
 
 
@@ -252,7 +342,12 @@
         rows = r1 - r0
         own = attend(q, k, v, ids, r0, r1)
         other = lax.ppermute(own, "dp", dp_pairs(swap=True))
-        (z_out,) = copies(send_kernel, [(CHIPS, rows, cols)], firsts, own, other)
+        direct = n in DIRECT
+        (z_out,) = copies(
+            send_kernel if direct else to_z_kernel,
+            [(CHIPS if direct else NZ * Z_SLOTS, rows, cols)],
+            firsts, own, other,
+        )
         if n == last:
             weight, _ = lax.optimization_barrier((out_weight, z_in))
             w_z = lax.all_to_all(
@@ -260,11 +355,25 @@
                 tiled=True, axis_index_groups=Z_GROUPS,
             )
             z_out, w_z = lax.optimization_barrier((z_out, w_z))
-        z_in = lax.all_to_all(z_out, "dp", 0, 0, tiled=True, axis_index_groups=CHIP_GROUPS)
-        (mine,) = copies(place_kernel, [(KEPT, rows, cols)], firsts, z_in)
+        groups = CHIP_GROUPS if direct else Z_GROUPS
+        z_in = lax.all_to_all(z_out, "dp", 0, 0, tiled=True, axis_index_groups=groups)
+        if direct:
+            (mine,) = copies(receive_kernel, [(KEPT, rows, cols)], firsts, z_in)
+        else:
+            y_out = copies(
+                to_y_kernel, [(Y_SLOTS, rows, cols)] * NY,
+                firsts, z_in,
+            )
+            y_in = [y_out[0]]
+            for t in range(1, NY):
+                y_in.append(lax.ppermute(y_out[t], "dp", dp_pairs(dy=t)))
+            (mine,) = copies(
+                place_kernel, [(KEPT, rows, cols)],
+                firsts, *y_in,
+            )
         left = lax.ppermute(mine, "mp", ring(4, 1))
         right = lax.ppermute(mine, "mp", ring(4, 3))
-        if n == last:
+        if n >= last - 2:
             far_a = lax.ppermute(left[:FIRST], "mp", ring(4, 1))
             far_b = lax.ppermute(right[FIRST:], "mp", ring(4, 3))
             results.append((mine, left, right, far_a, far_b))

time: 291 us -> 270 us (0.928)
  Pallas kernels: 71 us -> 57.6 us
  waiting for transfers between devices: 142 us -> 132 us
    ppermute x3, waiting for transfers between devices: 33.8 us -> 13.3 us  [step(): left = lax.ppermute(mine, 'mp', ring(4, 1))]
    ppermute x2 -> x9, waiting for transfers between devices: 8.41 us -> 27.7 us  [step(): y_in.append(lax.ppermute(y_out[t], 'dp', dp_pairs(dy=t)))]
    ppermute x3, waiting for transfers between devices: 29.2 us -> 18.9 us  [step(): right = lax.ppermute(mine, 'mp', ring(4, 3))]
    ppermute x1 -> x3, waiting for transfers between devices: 0.01 us -> 9.72 us  [step(): far_b = lax.ppermute(right[FIRST:], 'mp', ring(4, 3))]
    all_to_all x3, waiting for transfers between devices: 58.6 us -> 49.9 us  [step(): lax.all_to_all(z_out, 'dp', 0, 0, tiled=True, axis_index_groups=groups)]
    pallas_call x7 -> x10, Pallas kernels: 21.2 us -> 13.4 us  [copies(): pl.pallas_call(kernel, in_specs=[SMEM] + [VMEM] * len(operands), out_spec...]
    pallas_call x3, Pallas kernels: 25.4 us -> 18.5 us  [project(): pl.pallas_call(lambda *refs: project_kernel(halves, r0, *refs), in_specs=...]
    all_to_all x3, starting transfers between devices: 20.3 us -> 14 us  [step(): lax.all_to_all(z_out, 'dp', 0, 0, tiled=True, axis_index_groups=groups)]
  transfers between devices with their start and end apart: 25 -> 36, of which waited for: 10 -> 18; matrix products, arithmetic and copies ran while one was open for 1% -> 2% of each run, Pallas kernels for 18% -> 16%
where the time goes in v2:
time: 270 us; the launch traced here: 268 us
  waiting for transfers between devices  132 us (49%)
  starting transfers between devices  67.4 us (25%)
  Pallas kernels  57.6 us (21%)
  local copies, waits for them, and re-layouts  8.18 us (3%)
    all_to_all x3, waiting for transfers between devices, step(): lax.all_to_all(z_out, 'dp', 0, 0, tiled=True, axis_index_groups=groups)  49.9 us
    ppermute x9, waiting for transfers between devices, step(): y_in.append(lax.ppermute(y_out[t], 'dp', dp_pairs(dy=t)))  27.7 us
    pallas_call x3, Pallas kernels, attend(): pl.pallas_call(lambda *refs: attend_kernel(r0, r1, *refs), in_specs=[HBM,...  25.7 us
    ppermute x3, waiting for transfers between devices, step(): right = lax.ppermute(mine, 'mp', ring(4, 3))  18.9 us
    pallas_call x3, Pallas kernels, project(): pl.pallas_call(lambda *refs: project_kernel(halves, r0, *refs), in_specs=...  18.5 us
    all_to_all x3, starting transfers between devices, step(): lax.all_to_all(z_out, 'dp', 0, 0, tiled=True, axis_index_groups=groups)  14 us
    pallas_call x10, Pallas kernels, copies(): pl.pallas_call(kernel, in_specs=[SMEM] + [VMEM] * len(operands), out_spec...  13.4 us
    ppermute x3, waiting for transfers between devices, step(): left = lax.ppermute(mine, 'mp', ring(4, 1))  13.3 us
  transfers between devices with their start and end apart: 36, of which 18 were waited for; matrix products, arithmetic and copies ran while one was open for 2% of the time, Pallas kernels for 16%

profile of v2, /device:TPU:1, one launch (start us, length us, event | category | flops | bytes accessed | tf_op | source)
XLA Modules:
  0.0 268.0 jit_solution(14892992890767035663)
XLA Ops:
  0.0 7.9 %shard_map.66.own_ref = bf16[24,48,512]{2,1,0:T(8,128)(2,1)} custom-call(bf16[24,128,512]{2,1,0:T(8,128)(2,1)} %bitcast.7, bf16[24,128,128]{2,1,0:T(8,128)(2,1)} %bitcast.10, bf16[24,128,128]{2,1,0:T(8,128)(2,1)} %bitcast.13, s32[6,4,128]{2,1,0:T(4,128)} %bitcast.16), custom_call_target="tpu_custom_call" | custom-call | flops 226492416 | bytes 12582912 | tf_op jit(solution)/shard_map/pallas_call | solution.py:106
  7.9 3.3 %collective-permute-start.1 = (bf16[24,48,512]{2,1,0:T(8,128)(2,1)}, bf16[24,48,512]{2,1,0:T(8,128)(2,1)S(1)}, u32[]{:S(2)}, u32[]{:S(2)}) collective-permute-start(bf16[24,48,512]{2,1,0:T(8,128)(2,1)} %shard_map.66.own_ref), channel_id=1, source_target_pairs={{0,4},{4,0},{8,12},{12,8},{16,20},{20,16},{24,28},{28,24},{32,36},... | collective-permute-start | bytes 3538952 | tf_op jit(solution)/shard_map/ppermute | solution.py:344
  12.5 10.1 %all-to-all-start = ((s32[64,1,1]{2,1,0:T(1,128)}), s32[64,1,1]{2,1,0:T(1,128)S(1)}, u32[]{:S(2)}, u32[]{:S(2)}) async-start(s32[64,1,1]{2,1,0:T(1,128)} %broadcast_in_dim.40), calls=%async_computation | async-start | bytes 65536 | tf_op jit(solution)/shard_map/all_to_all | solution.py:324
  22.6 9.3 %all-to-all-done = s32[64,1,1]{2,1,0:T(1,128)S(1)} async-done(((s32[64,1,1]{2,1,0:T(1,128)}), s32[64,1,1]{2,1,0:T(1,128)S(1)}, u32[]{:S(2)}, u32[]{:S(2)}) %all-to-all-start) | async-done | bytes 288 | tf_op jit(solution)/shard_map/all_to_all | solution.py:324
  36.2 3.6 %all-to-all-start.1 = ((bf16[24,48,512]{2,1,0:T(8,128)(2,1)}), bf16[24,48,512]{2,1,0:T(8,128)(2,1)S(1)}, u32[]{:S(2)}, u32[]{:S(2)}) async-start(bf16[24,48,512]{2,1,0:T(8,128)(2,1)} %shard_map.67), calls=%async_computation.1 | async-start | bytes 2359296 | tf_op jit(solution)/shard_map/all_to_all | solution.py:359
  39.7 7.6 %shard_map.73.own_ref = bf16[24,48,512]{2,1,0:T(8,128)(2,1)} custom-call(bf16[24,128,512]{2,1,0:T(8,128)(2,1)} %bitcast.8, bf16[24,128,128]{2,1,0:T(8,128)(2,1)} %bitcast.11, bf16[24,128,128]{2,1,0:T(8,128)(2,1)} %bitcast.14, s32[6,4,128]{2,1,0:T(4,128)} %bitcast.17), custom_call_target="tpu_custom_call" | custom-call | flops 113246208 | bytes 12582912 | tf_op jit(solution)/shard_map/pallas_call | solution.py:106
  53.8 17.9 %all-to-all-done.1.in_ref = bf16[24,48,512]{2,1,0:T(8,128)(2,1)S(1)} async-done(((bf16[24,48,512]{2,1,0:T(8,128)(2,1)}), bf16[24,48,512]{2,1,0:T(8,128)(2,1)S(1)}, u32[]{:S(2)}, u32[]{:S(2)}) %all-to-all-start.1) | async-done | bytes 1179680 | tf_op jit(solution)/shard_map/all_to_all | solution.py:359
  71.7 3.6 %all-to-all-start.4 = ((bf16[24,48,512]{2,1,0:T(8,128)(2,1)}), bf16[24,48,512]{2,1,0:T(8,128)(2,1)S(1)}, u32[]{:S(2)}, u32[]{:S(2)}) async-start(bf16[24,48,512]{2,1,0:T(8,128)(2,1)} %shard_map.74), calls=%async_computation.4 | async-start | bytes 2359296 | tf_op jit(solution)/shard_map/all_to_all | solution.py:359
  75.3 32.0 %all-to-all-done.4.in_ref = bf16[24,48,512]{2,1,0:T(8,128)(2,1)S(1)} async-done(((bf16[24,48,512]{2,1,0:T(8,128)(2,1)}), bf16[24,48,512]{2,1,0:T(8,128)(2,1)S(1)}, u32[]{:S(2)}, u32[]{:S(2)}) %all-to-all-start.4) | async-done | bytes 1179680 | tf_op jit(solution)/shard_map/all_to_all | solution.py:359
  108.2 3.5 %all-to-all-start.2 = ((bf16[8,32,1024]{2,1,0:T(8,128)(2,1)}), bf16[8,32,1024]{2,1,0:T(8,128)(2,1)S(1)}, u32[]{:S(2)}, u32[]{:S(2)}) async-start(bf16[8,32,1024]{2,1,0:T(8,128)(2,1)} %broadcast_in_dim.44), calls=%async_computation.2 | async-start | bytes 1048576 | tf_op jit(solution)/shard_map/all_to_all | solution.py:353
  111.7 10.2 %shard_map.64.own_ref = bf16[24,32,512]{2,1,0:T(8,128)(2,1)} custom-call(bf16[24,128,512]{2,1,0:T(8,128)(2,1)} %bitcast.9, bf16[24,128,128]{2,1,0:T(8,128)(2,1)} %bitcast.12, bf16[24,128,128]{2,1,0:T(8,128)(2,1)} %bitcast.15, s32[6,4,128]{2,1,0:T(4,128)} %bitcast.18), custom_call_target="tpu_custom_call" | custom-call | flops 201326592 | bytes 12582912 | tf_op jit(solution)/shard_map/pallas_call | solution.py:106
  128.1 11.2 %collective-permute-done.24.rest_1_ = bf16[6,48,512]{2,1,0:T(8,128)(2,1)S(1)} collective-permute-done((bf16[6,48,512]{2,1,0:T(8,128)(2,1)S(1)}, bf16[6,48,512]{2,1,0:T(8,128)(2,1)S(1)}, u32[]{:S(2)}, u32[]{:S(2)}) %collective-permute-start.24) | collective-permute-done | bytes 294944 | tf_op jit(solution)/shard_map/ppermute | solution.py:369
  143.0 9.3 %collective-permute-done.16.rest_1_ = bf16[6,48,512]{2,1,0:T(8,128)(2,1)S(1)} collective-permute-done((bf16[6,48,512]{2,1,0:T(8,128)(2,1)S(1)}, bf16[6,48,512]{2,1,0:T(8,128)(2,1)S(1)}, u32[]{:S(2)}, u32[]{:S(2)}) %collective-permute-start.16) | collective-permute-done | bytes 294944 | tf_op jit(solution)/shard_map/ppermute | solution.py:369
  157.2 6.9 %all-to-all-start.3 = ((bf16[24,32,512]{2,1,0:T(8,128)(2,1)}), bf16[24,32,512]{2,1,0:T(8,128)(2,1)S(1)}, u32[]{:S(2)}, u32[]{:S(2)}) async-start(bf16[24,32,512]{2,1,0:T(8,128)(2,1)} %shard_map.65), calls=%async_computation.3 | async-start | bytes 1572864 | tf_op jit(solution)/shard_map/all_to_all | solution.py:359
  169.2 8.2 %collective-permute-done.28.refs_2_ = bf16[22,48,512]{2,1,0:T(8,128)(2,1)} collective-permute-done((bf16[22,48,512]{2,1,0:T(8,128)(2,1)}, bf16[22,48,512]{2,1,0:T(8,128)(2,1)}, u32[]{:S(2)}, u32[]{:S(2)}) %collective-permute-start.28) | collective-permute-done | bytes 1081376 | tf_op jit(solution)/shard_map/ppermute | solution.py:375
  177.4 12.6 %collective-permute-done.19.refs_1_ = bf16[22,48,512]{2,1,0:T(8,128)(2,1)S(1)} collective-permute-done((bf16[22,48,512]{2,1,0:T(8,128)(2,1)S(1)}, bf16[22,48,512]{2,1,0:T(8,128)(2,1)S(1)}, u32[]{:S(2)}, u32[]{:S(2)}) %collective-permute-start.19) | collective-permute-done | bytes 1081376 | tf_op jit(solution)/shard_map/ppermute | solution.py:374
  195.6 4.9 %collective-permute-done.20.refs_2_ = bf16[22,48,512]{2,1,0:T(8,128)(2,1)} collective-permute-done((bf16[22,48,512]{2,1,0:T(8,128)(2,1)S(1)}, bf16[22,48,512]{2,1,0:T(8,128)(2,1)}, u32[]{:S(2)}, u32[]{:S(2)}) %collective-permute-start.20) | collective-permute-done | bytes 1081376 | tf_op jit(solution)/shard_map/ppermute | solution.py:375
  206.6 6.5 %collective-permute-done.2.rest_1_ = bf16[6,32,512]{2,1,0:T(8,128)(2,1)S(1)} collective-permute-done((bf16[6,32,512]{2,1,0:T(8,128)(2,1)S(1)}, bf16[6,32,512]{2,1,0:T(8,128)(2,1)S(1)}, u32[]{:S(2)}, u32[]{:S(2)}) %collective-permute-start.2) | collective-permute-done | bytes 196640 | tf_op jit(solution)/shard_map/ppermute | solution.py:369
  229.0 7.6 %shard_map.77.refs_6_ = bf16[22,128,1024]{2,1,0:T(8,128)(2,1)} custom-call(bf16[22,48,512]{2,1,0:T(8,128)(2,1)} %shard_map.76.refs_0_, bf16[22,48,512]{2,1,0:T(8,128)(2,1)} %collective-permute-done.27.refs_1_, bf16[22,48,512]{2,1,0:T(8,128)(2,1)} %collective-permute-done.28.refs_2_, bf16[11,48,512]{2,1,0:T(8,128)(2,1)S(1)} %collective-permute-done.29.refs_3_, ...), custom_call_target="tpu_custom_call" | custom-call | flops 4429185024 | bytes 10682368 | tf_op jit(solution)/shard_map/pallas_call | solution.py:283
  238.6 5.9 %collective-permute-done.6.refs_2_ = bf16[22,32,512]{2,1,0:T(8,128)(2,1)S(1)} collective-permute-done((bf16[22,32,512]{2,1,0:T(8,128)(2,1)S(1)}, bf16[22,32,512]{2,1,0:T(8,128)(2,1)S(1)}, u32[]{:S(2)}, u32[]{:S(2)}) %collective-permute-start.6) | collective-permute-done | bytes 720928 | tf_op jit(solution)/shard_map/ppermute | solution.py:375
  244.5 3.5 %collective-permute-start.8 = (bf16[11,32,512]{2,1,0:T(8,128)(2,1)S(1)}, bf16[11,32,512]{2,1,0:T(8,128)(2,1)S(1)}, u32[]{:S(2)}, u32[]{:S(2)}) collective-permute-start(bf16[11,32,512]{2,1,0:T(8,128)(2,1)S(1)} %slice.25), channel_id=1, source_target_pairs={{0,3},{1,0},{2,1},{3,2},{4,7},{5,4},{6,5},{7,6},{8,11},{9,8},{10,9... | collective-permute-start | bytes 1081352 | tf_op jit(solution)/shard_map/ppermute | solution.py:378
  248.7 7.3 %collective-permute-done.22.refs_4_ = bf16[11,48,512]{2,1,0:T(8,128)(2,1)S(1)} collective-permute-done((bf16[11,48,512]{2,1,0:T(8,128)(2,1)S(1)}, bf16[11,48,512]{2,1,0:T(8,128)(2,1)S(1)}, u32[]{:S(2)}, u32[]{:S(2)}) %collective-permute-start.22) | collective-permute-done | bytes 540704 | tf_op jit(solution)/shard_map/ppermute | solution.py:378
  256.0 6.9 %shard_map.78.refs_6_ = bf16[22,128,1024]{2,1,0:T(8,128)(2,1)} custom-call(bf16[22,48,512]{2,1,0:T(8,128)(2,1)S(1)} %shard_map.72.refs_0_, bf16[22,48,512]{2,1,0:T(8,128)(2,1)S(1)} %collective-permute-done.19.refs_1_, bf16[22,48,512]{2,1,0:T(8,128)(2,1)} %collective-permute-done.20.refs_2_, ...), custom_call_target="tpu_custom_call", output_to_operand_aliasing={{}: (6, {})} | custom-call | flops 4429185024 | bytes 10682368 | tf_op jit(solution)/shard_map/pallas_call | solution.py:283
  263.8 4.0 %shard_map.79 = bf16[22,128,1024]{2,1,0:T(8,128)(2,1)} custom-call(bf16[22,32,512]{2,1,0:T(8,128)(2,1)S(1)} %shard_map.69.refs_0_, bf16[22,32,512]{2,1,0:T(8,128)(2,1)S(1)} %collective-permute-done.5.refs_1_, bf16[22,32,512]{2,1,0:T(8,128)(2,1)S(1)} %collective-permute-done.6.refs_2_, ...), custom_call_target="tpu_custom_call", output_to_operand_aliasing={{}: (6, {})} | custom-call | flops 2952790016 | bytes 8519680 | tf_op jit(solution)/shard_map/pallas_call | solution.py:283
  (83 shorter events, 63.2 us)
Async XLA Ops:
  7.9 25.3 %collective-permute-start.1 = (bf16[24,48,512]{2,1,0:T(8,128)(2,1)}, bf16[24,48,512]{2,1,0:T(8,128)(2,1)S(1)}, u32[]{:S(2)}, u32[]{:S(2)}) collective-permute-start(bf16[24,48,512]{2,1,0:T(8,128)(2,1)} %shard_map.66.own_ref), channel_id=1, source_target_pairs={{0,4},{4,0},{8,12},{12,8},{16,20},{20,16},{24,28},{28,24},{32,36},... | collective-permute-start | bytes 3538952 | tf_op jit(solution)/shard_map/ppermute | solution.py:344
  12.5 19.4 %all-to-all-start = ((s32[64,1,1]{2,1,0:T(1,128)}), s32[64,1,1]{2,1,0:T(1,128)S(1)}, u32[]{:S(2)}, u32[]{:S(2)}) async-start(s32[64,1,1]{2,1,0:T(1,128)} %broadcast_in_dim.40), calls=%async_computation | async-start | bytes 65536 | tf_op jit(solution)/shard_map/all_to_all | solution.py:324
  36.2 35.6 %all-to-all-start.1 = ((bf16[24,48,512]{2,1,0:T(8,128)(2,1)}), bf16[24,48,512]{2,1,0:T(8,128)(2,1)S(1)}, u32[]{:S(2)}, u32[]{:S(2)}) async-start(bf16[24,48,512]{2,1,0:T(8,128)(2,1)} %shard_map.67), calls=%async_computation.1 | async-start | bytes 2359296 | tf_op jit(solution)/shard_map/all_to_all | solution.py:359
  71.7 35.5 %all-to-all-start.4 = ((bf16[24,48,512]{2,1,0:T(8,128)(2,1)}), bf16[24,48,512]{2,1,0:T(8,128)(2,1)S(1)}, u32[]{:S(2)}, u32[]{:S(2)}) async-start(bf16[24,48,512]{2,1,0:T(8,128)(2,1)} %shard_map.74), calls=%async_computation.4 | async-start | bytes 2359296 | tf_op jit(solution)/shard_map/all_to_all | solution.py:359
  108.2 49.1 %all-to-all-start.2 = ((bf16[8,32,1024]{2,1,0:T(8,128)(2,1)}), bf16[8,32,1024]{2,1,0:T(8,128)(2,1)S(1)}, u32[]{:S(2)}, u32[]{:S(2)}) async-start(bf16[8,32,1024]{2,1,0:T(8,128)(2,1)} %broadcast_in_dim.44), calls=%async_computation.2 | async-start | bytes 1048576 | tf_op jit(solution)/shard_map/all_to_all | solution.py:353
  121.8 33.9 %collective-permute-start = (bf16[24,32,512]{2,1,0:T(8,128)(2,1)}, bf16[24,32,512]{2,1,0:T(8,128)(2,1)S(1)}, u32[]{:S(2)}, u32[]{:S(2)}) collective-permute-start(bf16[24,32,512]{2,1,0:T(8,128)(2,1)} %shard_map.64.own_ref), channel_id=1, source_target_pairs={{0,4},{4,0},{8,12},{12,8},{16,20},{20,16},{24,28},{28,24},{32,36},... | collective-permute-start | bytes 2359304 | tf_op jit(solution)/shard_map/ppermute | solution.py:344
  123.4 15.9 %collective-permute-start.24 = (bf16[6,48,512]{2,1,0:T(8,128)(2,1)S(1)}, bf16[6,48,512]{2,1,0:T(8,128)(2,1)S(1)}, u32[]{:S(2)}, u32[]{:S(2)}) collective-permute-start(bf16[6,48,512]{2,1,0:T(8,128)(2,1)S(1)} %get-tuple-element.32), channel_id=1, source_target_pairs={{0,64},{4,68},{8,72},{12,76},{16,80},{20,84},{24,88},{28,92},{32,9... | collective-permute-start | bytes 884744 | tf_op jit(solution)/shard_map/ppermute | solution.py:369
  127.7 24.6 %collective-permute-start.16 = (bf16[6,48,512]{2,1,0:T(8,128)(2,1)S(1)}, bf16[6,48,512]{2,1,0:T(8,128)(2,1)S(1)}, u32[]{:S(2)}, u32[]{:S(2)}) collective-permute-start(bf16[6,48,512]{2,1,0:T(8,128)(2,1)S(1)} %get-tuple-element.28), channel_id=1, source_target_pairs={{0,64},{4,68},{8,72},{12,76},{16,80},{20,84},{24,88},{28,92},{32,9... | collective-permute-start | bytes 884744 | tf_op jit(solution)/shard_map/ppermute | solution.py:369
  141.8 25.0 %collective-permute-start.27 = (bf16[22,48,512]{2,1,0:T(8,128)(2,1)}, bf16[22,48,512]{2,1,0:T(8,128)(2,1)}, u32[]{:S(2)}, u32[]{:S(2)}) collective-permute-start(bf16[22,48,512]{2,1,0:T(8,128)(2,1)} %shard_map.76.refs_0_), channel_id=1, source_target_pairs={{0,1},{1,2},{2,3},{3,0},{4,5},{5,6},{6,7},{7,4},{8,9},{9,10},{10,1... | collective-permute-start | bytes 3244040 | tf_op jit(solution)/shard_map/ppermute | solution.py:374
  152.3 25.0 %collective-permute-start.28 = (bf16[22,48,512]{2,1,0:T(8,128)(2,1)}, bf16[22,48,512]{2,1,0:T(8,128)(2,1)}, u32[]{:S(2)}, u32[]{:S(2)}) collective-permute-start(bf16[22,48,512]{2,1,0:T(8,128)(2,1)} %shard_map.76.refs_0_), channel_id=1, source_target_pairs={{0,3},{1,0},{2,1},{3,2},{4,7},{5,4},{6,5},{7,6},{8,11},{9,8},{10,9... | collective-permute-start | bytes 3244040 | tf_op jit(solution)/shard_map/ppermute | solution.py:375
  155.6 34.4 %collective-permute-start.19 = (bf16[22,48,512]{2,1,0:T(8,128)(2,1)S(1)}, bf16[22,48,512]{2,1,0:T(8,128)(2,1)S(1)}, u32[]{:S(2)}, u32[]{:S(2)}) collective-permute-start(bf16[22,48,512]{2,1,0:T(8,128)(2,1)S(1)} %shard_map.72.refs_0_), channel_id=1, source_target_pairs={{0,1},{1,2},{2,3},{3,0},{4,5},{5,6},{6,7},{7,4},{8,9},{9,10},{10,1... | collective-permute-start | bytes 3244040 | tf_op jit(solution)/shard_map/ppermute | solution.py:374
  157.2 37.3 %all-to-all-start.3 = ((bf16[24,32,512]{2,1,0:T(8,128)(2,1)}), bf16[24,32,512]{2,1,0:T(8,128)(2,1)S(1)}, u32[]{:S(2)}, u32[]{:S(2)}) async-start(bf16[24,32,512]{2,1,0:T(8,128)(2,1)} %shard_map.65), calls=%async_computation.3 | async-start | bytes 1572864 | tf_op jit(solution)/shard_map/all_to_all | solution.py:359
  164.1 36.4 %collective-permute-start.20 = (bf16[22,48,512]{2,1,0:T(8,128)(2,1)S(1)}, bf16[22,48,512]{2,1,0:T(8,128)(2,1)}, u32[]{:S(2)}, u32[]{:S(2)}) collective-permute-start(bf16[22,48,512]{2,1,0:T(8,128)(2,1)S(1)} %shard_map.72.refs_0_), channel_id=1, source_target_pairs={{0,3},{1,0},{2,1},{3,2},{4,7},{5,4},{6,5},{7,6},{8,11},{9,8},{10,9... | collective-permute-start | bytes 3244040 | tf_op jit(solution)/shard_map/ppermute | solution.py:375
  166.7 34.7 %collective-permute-start.9 = (bf16[8,32,1024]{2,1,0:T(8,128)(2,1)S(1)}, bf16[8,32,1024]{2,1,0:T(8,128)(2,1)}, u32[]{:S(2)}, u32[]{:S(2)}) collective-permute-start(bf16[8,32,1024]{2,1,0:T(8,128)(2,1)S(1)} %all-to-all-done.2.rest_0_), channel_id=1, source_target_pairs={{0,64},{4,68},{8,72},{12,76},{16,80},{20,84},{24,88},{28,92},{32,9... | collective-permute-start | bytes 1572872 | tf_op jit(solution)/shard_map/ppermute | solution.py:385
  166.8 34.7 %collective-permute-start.10 = (bf16[8,32,1024]{2,1,0:T(8,128)(2,1)S(1)}, bf16[8,32,1024]{2,1,0:T(8,128)(2,1)}, u32[]{:S(2)}, u32[]{:S(2)}) collective-permute-start(bf16[8,32,1024]{2,1,0:T(8,128)(2,1)S(1)} %all-to-all-done.2.rest_0_), channel_id=1, source_target_pairs={{0,128},{4,132},{8,136},{12,140},{16,144},{20,148},{24,152},{28,15... | collective-permute-start | bytes 1572872 | tf_op jit(solution)/shard_map/ppermute | solution.py:385
  177.4 24.2 %collective-permute-start.11 = (bf16[8,32,1024]{2,1,0:T(8,128)(2,1)S(1)}, bf16[8,32,1024]{2,1,0:T(8,128)(2,1)}, u32[]{:S(2)}, u32[]{:S(2)}) collective-permute-start(bf16[8,32,1024]{2,1,0:T(8,128)(2,1)S(1)} %all-to-all-done.2.rest_0_), channel_id=1, source_target_pairs={{0,192},{4,196},{8,200},{12,204},{16,208},{20,212},{24,216},{28,22... | collective-permute-start | bytes 1572872 | tf_op jit(solution)/shard_map/ppermute | solution.py:385
  200.5 18.2 %collective-permute-start.29 = (bf16[11,48,512]{2,1,0:T(8,128)(2,1)}, bf16[11,48,512]{2,1,0:T(8,128)(2,1)S(1)}, u32[]{:S(2)}, u32[]{:S(2)}) collective-permute-start(bf16[11,48,512]{2,1,0:T(8,128)(2,1)} %slice.28), channel_id=1, source_target_pairs={{0,1},{1,2},{2,3},{3,0},{4,5},{5,6},{6,7},{7,4},{8,9},{9,10},{10,1... | collective-permute-start | bytes 1622024 | tf_op jit(solution)/shard_map/ppermute | solution.py:377
  201.6 17.4 %collective-permute-start.13 = (bf16[8,32,1024]{2,1,0:T(8,128)(2,1)}, bf16[8,32,1024]{2,1,0:T(8,128)(2,1)S(1)}, u32[]{:S(2)}, u32[]{:S(2)}) collective-permute-start(bf16[8,32,1024]{2,1,0:T(8,128)(2,1)} %collective-permute-done.9.rest_1_), channel_id=1, source_target_pairs={{0,4},{4,0},{8,12},{12,8},{16,20},{20,16},{24,28},{28,24},{32,36},... | collective-permute-start | bytes 1572872 | tf_op jit(solution)/shard_map/ppermute | solution.py:387
  218.7 18.4 %collective-permute-start.5 = (bf16[22,32,512]{2,1,0:T(8,128)(2,1)S(1)}, bf16[22,32,512]{2,1,0:T(8,128)(2,1)S(1)}, u32[]{:S(2)}, u32[]{:S(2)}) collective-permute-start(bf16[22,32,512]{2,1,0:T(8,128)(2,1)S(1)} %shard_map.69.refs_0_), channel_id=1, source_target_pairs={{0,1},{1,2},{2,3},{3,0},{4,5},{5,6},{6,7},{7,4},{8,9},{9,10},{10,1... | collective-permute-start | bytes 2162696 | tf_op jit(solution)/shard_map/ppermute | solution.py:374
  219.0 25.4 %collective-permute-start.6 = (bf16[22,32,512]{2,1,0:T(8,128)(2,1)S(1)}, bf16[22,32,512]{2,1,0:T(8,128)(2,1)S(1)}, u32[]{:S(2)}, u32[]{:S(2)}) collective-permute-start(bf16[22,32,512]{2,1,0:T(8,128)(2,1)S(1)} %shard_map.69.refs_0_), channel_id=1, source_target_pairs={{0,3},{1,0},{2,1},{3,2},{4,7},{5,4},{6,5},{7,6},{8,11},{9,8},{10,9... | collective-permute-start | bytes 2162696 | tf_op jit(solution)/shard_map/ppermute | solution.py:375
  222.8 25.9 %collective-permute-start.21 = (bf16[11,48,512]{2,1,0:T(8,128)(2,1)S(1)}, bf16[11,48,512]{2,1,0:T(8,128)(2,1)S(1)}, u32[]{:S(2)}, u32[]{:S(2)}) collective-permute-start(bf16[11,48,512]{2,1,0:T(8,128)(2,1)S(1)} %slice.26), channel_id=1, source_target_pairs={{0,1},{1,2},{2,3},{3,0},{4,5},{5,6},{6,7},{7,4},{8,9},{9,10},{10,1... | collective-permute-start | bytes 1622024 | tf_op jit(solution)/shard_map/ppermute | solution.py:377
  222.9 33.1 %collective-permute-start.22 = (bf16[11,48,512]{2,1,0:T(8,128)(2,1)S(1)}, bf16[11,48,512]{2,1,0:T(8,128)(2,1)S(1)}, u32[]{:S(2)}, u32[]{:S(2)}) collective-permute-start(bf16[11,48,512]{2,1,0:T(8,128)(2,1)S(1)} %slice.27), channel_id=1, source_target_pairs={{0,3},{1,0},{2,1},{3,2},{4,7},{5,4},{6,5},{7,6},{8,11},{9,8},{10,9... | collective-permute-start | bytes 1622024 | tf_op jit(solution)/shard_map/ppermute | solution.py:378
  237.2 25.8 %collective-permute-start.7 = (bf16[11,32,512]{2,1,0:T(8,128)(2,1)S(1)}, bf16[11,32,512]{2,1,0:T(8,128)(2,1)S(1)}, u32[]{:S(2)}, u32[]{:S(2)}) collective-permute-start(bf16[11,32,512]{2,1,0:T(8,128)(2,1)S(1)} %slice.24), channel_id=1, source_target_pairs={{0,1},{1,2},{2,3},{3,0},{4,5},{5,6},{6,7},{7,4},{8,9},{9,10},{10,1... | collective-permute-start | bytes 1081352 | tf_op jit(solution)/shard_map/ppermute | solution.py:377
  244.5 19.3 %collective-permute-start.8 = (bf16[11,32,512]{2,1,0:T(8,128)(2,1)S(1)}, bf16[11,32,512]{2,1,0:T(8,128)(2,1)S(1)}, u32[]{:S(2)}, u32[]{:S(2)}) collective-permute-start(bf16[11,32,512]{2,1,0:T(8,128)(2,1)S(1)} %slice.25), channel_id=1, source_target_pairs={{0,3},{1,0},{2,1},{3,2},{4,7},{5,4},{6,5},{7,6},{8,11},{9,8},{10,9... | collective-permute-start | bytes 1081352 | tf_op jit(solution)/shard_map/ppermute | solution.py:378
  (16 other events, 215.8 us)
